TPU v7x, 256 devices: a whole 4x4x8 slice. The times are simulated.
256 devices in a mesh: img: 16 (over x, z_lo, core), tp: 16 (over y, z_hi).
Axes of the slice: x: 4, y: 4, z: 8 (z_hi: 4, z_lo: 2; z = z_hi * 2 + z_lo), core: 2. Of those that a mesh axis runs over, the one named last changes fastest.
Arguments:
- patch_tokens: bfloat16 [32768, 1024], P(('img', 'tp')), may hold values from -12 to 12
- norm_gain: float32 [1024], replicated, may hold values from 0.1 to 1.9
- norm_bias: float32 [1024], replicated, may hold values from -3 to 3
- up_weight: bfloat16 [1024, 8192], P('img', 'tp'), may hold values from -0.1875 to 0.1875
- up_bias: float32 [8192], P('tp'), may hold values from -3 to 3
- down_weight: bfloat16 [8192, 4096], P('tp', 'img'), may hold values from -0.125 to 0.125
- down_bias: float32 [4096], replicated, may hold values from -3 to 3
Outputs:
- projected: bfloat16 [32768, 4096], P(('img', 'tp'))
All inputs are finite; a program needn't handle non-finite values.
Results may differ from a plain program's by a relative error of at most 0.014.
Values may be sent and summed in bfloat16 or wider, within the bound.
No kernel may reach another device: no remote copies, remote signals or barrier semaphores. Data moves between devices by JAX's collectives and lax.ppermute only.
A program may use at most 128 MiB of HBM per device.

v0:
```python
import functools

import jax
import jax.numpy as jnp
from jax import lax
from jax.experimental import pallas as pl
from jax.experimental.pallas import tpu as pltpu
from jax.sharding import Mesh
from jax.sharding import PartitionSpec as P


BF = jnp.bfloat16
F32 = jnp.float32
D, TOK = 1024, 128
X, Y, Z, ZH = 4, 4, 8, 4
GROUP = 512
COLS = 256
HID = ZH * GROUP
NX = 4 * COLS
ANY = pl.BlockSpec(memory_space=pl.ANY)
VMEM = pl.BlockSpec(memory_space=pltpu.VMEM)


def ring(n, d):
    return [(i, (i + d) % n) for i in range(n)]


def both_ways(n):
    return [(2 * i + c, 2 * ((i + (1 - 2 * c)) % n) + c) for i in range(n) for c in (0, 1)]


def on_x(a, d):
    return lax.ppermute(a, "x", ring(X, d))


def on_y(a, d):
    return lax.ppermute(a, "y", ring(Y, d))


def on_z(a):
    def at(i):
        return (i // 2 % 2 * 2 + i % 2) * ZH + i // 4

    return lax.ppermute(a, ("zl", "c", "zh"), [(at(i), at(j)) for i, j in both_ways(Z)])


def over_z(a):
    return lax.all_to_all(a, ("zl", "zh"), split_axis=0, concat_axis=0, tiled=True)


def on_xc(a):
    return lax.ppermute(a, ("x", "c"), both_ways(X))


def on_c(a):
    return lax.ppermute(a, "c", [(0, 1), (1, 0)])


def norm_kernel(x_ref, g_ref, b_ref, o_ref):
    @pl.loop(0, 4)
    def _(i):
        rows = pl.ds(pl.multiple_of(i * 32, 32), 32)
        v = x_ref[rows].astype(F32)
        center = jnp.mean(v, axis=1, keepdims=True)
        w = v - center
        spread = jnp.mean(w * w, axis=1, keepdims=True)
        o_ref[rows] = (w * lax.rsqrt(spread + 1e-05) * g_ref[...] + b_ref[...]).astype(BF)


def normalize(rows, gain, bias):
    return pl.pallas_call(
        norm_kernel,
        out_shape=jax.ShapeDtypeStruct(rows.shape, BF),
        in_specs=[VMEM] * 3,
        out_specs=VMEM,
        compiler_params=pltpu.CompilerParams(vmem_limit_bytes=8 * 2**20),
        name="norm",
        cost_estimate=pl.CostEstimate(flops=10**6, bytes_accessed=2**19, transcendentals=128),
    )(rows, gain[None], bias[None])


def side(c):
    return 2 * c - 1


UP_EARLY, UP_LATE = ("f", "g", "x1f", "x1g", "ex1f"), ("ex1g", "x2f", "ex2f")
DOWN_EARLY, DOWN_LATE = ("w0", "e0", "w1", "w2", "e1", "e2", "w3"), ("e3", "w4", "e4")
BIASES = ("w0", "w1", "w2", "w3", "w4", "e1", "e2", "e3", "e4")


def place_kernel(ups, downs, biases, n_old, *refs):
    n = len(ups) + len(downs) + len(biases)
    pieces = dict(zip(ups + downs + biases, refs))
    up_out, down_out, *bias_out, part, sem = refs[n + n_old :]
    x, c = lax.axis_index("x"), lax.axis_index("c")
    z = lax.axis_index("zh") * 2 + lax.axis_index("zl")
    o = 1 - c
    copies = []

    def copy(src, dst):
        cp = pltpu.make_async_copy(src, dst, sem)
        cp.start()
        copies.append(cp)

    def xs(d):
        return lax.rem(x + d + X, X)

    def put(src, zz, cc):
        row = pl.multiple_of(lax.div(zz, 2) * GROUP, GROUP)
        copy(src, down_out.at[lax.rem(zz, 2) * 2 + cc, pl.ds(row, GROUP)])

    def source(name):
        s, k = int(name[1]), c if name[0] == "w" else o
        return pieces[name], s, k, lax.rem(z + s * side(k) + Z, Z)

    for name in downs:
        ref, s, k, zz = source(name)
        put(ref.at[:GROUP], zz, k)
        if 0 < s < 4:
            put(ref.at[pl.ds(GROUP + 8, GROUP)], zz, 1 - k)
    for i, name in enumerate(biases):
        copy(source(name)[0].at[pl.ds(GROUP, 8)], part.at[i])
    where = {
        "f": (x, c), "g": (x, o),
        "x1f": (xs(side(c)), c), "x1g": (xs(side(c)), o),
        "ex1f": (xs(side(o)), o), "ex1g": (xs(side(o)), c),
        "x2f": (xs(2), c), "x2g": (xs(2), o), "ex2f": (xs(2), o),
    }
    for name in ups:
        xx, k = where[name]
        for zl in range(2):
            row = pl.multiple_of(((xx * 2 + zl) * 2 + k) * 64, 64)
            copy(pieces[name].at[zl * ZH : (zl + 1) * ZH], up_out.at[:, pl.ds(row, 64)])
    for cp in copies:
        cp.wait()
    for i, name in enumerate(biases):
        v = part[i].astype(F32)
        row = pl.ds(lax.div(source(name)[3], 2), 1)
        for k in range(2):
            b = v[k : k + 1] + v[2 + k : 3 + k] + v[4 + k : 5 + k]
            bias_out[0][row, k * COLS : (k + 1) * COLS] = b


def place(ups, downs, biases, values, old=()):
    n = len(ups) + len(downs) + len(biases)
    more = (jax.ShapeDtypeStruct((ZH, GROUP), F32),) if biases else ()
    return pl.pallas_call(
        functools.partial(place_kernel, ups, downs, biases, len(old)),
        out_shape=(
            jax.ShapeDtypeStruct((ZH, D, GROUP), BF),
            jax.ShapeDtypeStruct((4, HID, COLS), BF),
            *more,
        ),
        in_specs=[ANY] * (n + len(old)),
        out_specs=(ANY, ANY) + (VMEM,) * len(more),
        scratch_shapes=[pltpu.VMEM((9, 8, COLS), BF), pltpu.SemaphoreType.DMA],
        input_output_aliases={n + i: i for i in range(len(old))},
        compiler_params=pltpu.CompilerParams(vmem_limit_bytes=2 * 2**20),
        cost_estimate=pl.CostEstimate(flops=10**6, bytes_accessed=2**23, transcendentals=0),
    )(*[values[k] for k in ups + downs + biases], *old)


def split_kernel(b_ref, o_ref):
    b = jnp.concatenate([b_ref[:, :COLS], b_ref[:, COLS:]], axis=0)
    hi = b.astype(BF)
    rest = b - hi.astype(F32)
    mid = rest.astype(BF)
    low = (rest - mid.astype(F32)).astype(BF)
    o_ref[...] = jnp.concatenate([hi, mid, low, jnp.zeros_like(low)], axis=0)


def split_bias(b):
    return pl.pallas_call(
        split_kernel,
        out_shape=jax.ShapeDtypeStruct((8, COLS), BF),
        in_specs=[VMEM],
        out_specs=VMEM,
        compiler_params=pltpu.CompilerParams(vmem_limit_bytes=8 * 2**20),
        name="split_bias",
    )(b[None])


def mlp_kernel(plan, *refs):
    toks, (up, bias, down), outs, (t_ref, h_ref) = (
        refs[:-7], refs[-7:-4], refs[-4:-2], refs[-2:],
    )
    for t, parts in zip(toks, plan):
        for src, dst, n in parts:
            t_ref[dst : dst + n] = t[src : src + n]

    @pl.loop(0, 2)
    def _(i):
        rows = pl.ds(pl.multiple_of(i * 256, 256), 256)
        for g in range(ZH):
            s = jnp.dot(t_ref[rows], up[g], preferred_element_type=F32) + bias[g : g + 1]
            h_ref[:, g * GROUP : (g + 1) * GROUP] = jax.nn.gelu(s).astype(BF)
        for j in range(4):
            o = jnp.dot(h_ref[...], down[j], preferred_element_type=F32)
            outs[j % 2][j // 2, rows] = o.astype(BF)


def small_mlp_kernel(*refs):
    toks, (up, bias, down), outs, (t_ref, h_ref) = (
        refs[:-7], refs[-7:-4], refs[-4:-2], refs[-2:],
    )
    t_ref[0:128] = toks[0][...]
    t_ref[128:512] = toks[1][...]

    @pl.loop(0, 2)
    def _(i):
        rows = pl.ds(pl.multiple_of(i * 256, 256), 256)

        @pl.loop(0, ZH)
        def _(g):
            s = jnp.dot(t_ref[rows], up[g], preferred_element_type=F32) + bias[pl.ds(g, 1)]
            h_ref[:, pl.ds(pl.multiple_of(g * GROUP, GROUP), GROUP)] = jax.nn.gelu(s).astype(BF)

        @pl.loop(0, 2)
        def _(h):
            for j in range(2):
                o = jnp.dot(h_ref[...], down[2 * h + j], preferred_element_type=F32)
                outs[j][h, rows] = o.astype(BF)


def mlp(toks, plan, up, bias, down, small=False):
    rows = 512
    half = jax.ShapeDtypeStruct((2, rows, COLS), BF)
    return pl.pallas_call(
        small_mlp_kernel if small else functools.partial(mlp_kernel, plan),
        out_shape=(half, half),
        in_specs=[VMEM] * (len(toks) + 3),
        out_specs=(VMEM, VMEM),
        scratch_shapes=[pltpu.VMEM((rows, D), BF), pltpu.VMEM((256, HID), BF)],
        compiler_params=pltpu.CompilerParams(vmem_limit_bytes=20 * 2**20),
        name="mlp",
        cost_estimate=pl.CostEstimate(
            flops=10**8, bytes_accessed=2**23, transcendentals=rows * HID
        ),
    )(*toks, up, bias, down)


def add_kernel(h, p_ref, r_ref, o_ref):
    @pl.loop(0, 4)
    def _(i):
        rows = pl.ds(pl.multiple_of(i * TOK, TOK), TOK)
        o_ref[rows] = (p_ref[h, rows].astype(F32) + r_ref[h, rows].astype(F32)).astype(BF)


def add_in(p, r, h):
    return pl.pallas_call(
        functools.partial(add_kernel, h),
        out_shape=jax.ShapeDtypeStruct(p.shape[1:], BF),
        in_specs=[VMEM] * 2,
        out_specs=VMEM,
        compiler_params=pltpu.CompilerParams(vmem_limit_bytes=8 * 2**20),
        name="add_in",
        cost_estimate=pl.CostEstimate(flops=10**6, bytes_accessed=2**20, transcendentals=0),
    )(p, r)


def sum_kernel(h, p0, p1, sum0, one0, one1, sum1, bias_ref, *outs):
    x = lax.axis_index("x")

    @pl.loop(0, 4)
    def _(r):
        to = pl.ds(pl.multiple_of(r * 32, 32), 32)
        for i, o in enumerate(outs):
            rows = pl.ds(pl.multiple_of(i * TOK + r * 32, 32), 32)
            for j, (p, full, part) in enumerate(((p0, sum0, one0), (p1, sum1, one1))):
                cols = pl.ds(pl.multiple_of(x * NX + (2 * h + j) * COLS, COLS), COLS)
                v = p[h, rows].astype(F32) + full[rows].astype(F32) + part[h, rows].astype(F32)
                o[j, to] = (v + bias_ref[:, cols]).astype(BF)


def sum_up(h, *values):
    return pl.pallas_call(
        functools.partial(sum_kernel, h),
        out_shape=(jax.ShapeDtypeStruct((2, TOK, COLS), BF),) * 4,
        in_specs=[VMEM] * 7,
        out_specs=(VMEM,) * 4,
        compiler_params=pltpu.CompilerParams(vmem_limit_bytes=8 * 2**20),
        name="sum_up",
        cost_estimate=pl.CostEstimate(flops=10**6, bytes_accessed=2**20, transcendentals=0),
    )(*values)


def out_kernel(*refs):
    pieces, o_ref, sem = refs[:-2], refs[-2], refs[-1]
    x = lax.axis_index("x")
    copies = []
    for i, ref in enumerate(pieces):
        h, r = divmod(i, 4)
        xx = lax.rem(x + (0, X - 1, 1, 2)[r], X)
        for j in range(2):
            col = pl.multiple_of(xx * NX + h * 512 + j * 256, 256)
            cp = pltpu.make_async_copy(ref.at[j], o_ref.at[:, pl.ds(col, COLS)], sem)
            cp.start()
            copies.append(cp)
    for cp in copies:
        cp.wait()


def put_out(pieces):
    return pl.pallas_call(
        out_kernel,
        out_shape=jax.ShapeDtypeStruct((TOK, X * NX), BF),
        in_specs=[VMEM] * len(pieces),
        out_specs=ANY,
        scratch_shapes=[pltpu.SemaphoreType.DMA],
        compiler_params=pltpu.CompilerParams(vmem_limit_bytes=8 * 2**20),
        name="put_out",
    )(*pieces)


def step(patch_tokens, norm_gain, norm_bias, up_weight, up_bias, down_weight, down_bias):
    own = normalize(patch_tokens, norm_gain, norm_bias)
    left, right = on_x(own, 1), on_x(own, -1)
    below = [on_y(own, 1)]
    above = [on_y(own, -1)]
    rest = jnp.concatenate([left, right, on_x(own, 2)], axis=0)
    below.append(on_y(rest, 1))
    above.append(on_y(rest, -1))
    half0 = jnp.concatenate([below[0][:64], below[1][:192]], axis=0)
    half1 = jnp.concatenate([above[0][64:], above[1][192:]], axis=0)
    far = [on_y(half0, 1), on_y(half1, -1)]

    copies = jnp.broadcast_to(up_weight, (Z, *up_weight.shape))
    f = over_z(copies)
    g = on_c(f)
    x1f, x1g = on_xc(f), on_xc(g)
    x2f = on_xc(x1f)
    pieces = dict(f=f, g=g, x1f=x1f, x1g=x1g, x2f=x2f, ex1f=on_c(x1f))
    pieces |= dict(ex1g=on_c(x1g), ex2f=on_c(x2f))

    d_other = on_c(down_weight)
    w = [jnp.concatenate([down_weight, split_bias(up_bias), d_other], axis=0)]
    for _ in range(3):
        w.append(on_z(w[-1]))
    w.append(on_z(w[3][: GROUP + 8]))
    pieces |= dict(w0=w[0], e0=d_other)
    for k, a in enumerate(w[1:], 1):
        pieces |= {f"w{k}": a, f"e{k}": on_c(a)}

    early = place(UP_EARLY, DOWN_EARLY, (), pieces)
    up, down, bias = place(UP_LATE, DOWN_LATE, BIASES, pieces, early)
    halves = (((0, 0, 64), (64, 128, 192)), ((0, 64, 64), (64, 320, 192)))
    wholes = (((0, 0, 128),), ((0, 128, 384),))
    far0, far1 = mlp(far, halves, up, bias, down)
    from_below, from_above = on_y(far0, 1), on_y(far1, -1)
    above0, above1 = mlp(above, wholes, up, bias, down)
    one1 = on_y(above1, 1)
    below0, below1 = mlp(below, wholes, up, bias, down)
    one0 = on_y(below0, -1)
    own0, own1 = mlp([own, rest], wholes, up, bias, down, True)
    placed = []
    for h in range(2):
        sum0 = on_y(add_in(above0, from_below, h), 1)
        sum1 = on_y(add_in(below1, from_above, h), -1)
        values = (own0, own1, sum0, one0, one1, sum1, down_bias[None])
        mine, to_left, to_right, to_far = sum_up(h, *values)
        opposite = on_x(to_far, 2)
        placed += [mine, on_x(to_right, 1), on_x(to_left, -1), opposite]
    return put_out(placed)


def solution(mesh):
    grid = Mesh(mesh.devices.reshape(X, 2, 2, Y, ZH), ("x", "zl", "c", "y", "zh"))
    img, tp = ("x", "zl", "c"), ("y", "zh")
    return jax.shard_map(
        step,
        mesh=grid,
        in_specs=(P((*img, *tp), None), P(), P(), P(img, tp), P(tp), P(tp, img), P()),
        out_specs=P((*img, *tp), None),
        check_vma=False,
    )
```

profile of v0, /device:TPU:16, one launch (start us, length us, event | category | flops | bytes accessed | tf_op | source)
XLA Modules:
  0.0 152.5 jit_solution(17795177421483332013)
XLA Ops:
  4.7 1.7 %collective-permute-start.1 = (bf16[128,1024]{1,0:T(8,128)(2,1)S(1)}, bf16[128,1024]{1,0:T(8,128)(2,1)S(1)}, u32[]{:S(2)}, u32[]{:S(2)}) collective-permute-start(bf16[128,1024]{1,0:T(8,128)(2,1)S(1)} %norm.1.refs_0_), channel_id=1, source_target_pairs={{0,192},{64,0},{128,64},{192,128},{1,193},{65,1},{129,65},{193,129... | collective-permute-start | bytes 786440 | tf_op jit(solution)/shard_map/ppermute | solution.py:33
  6.4 1.8 %collective-permute-start.2 = (bf16[128,1024]{1,0:T(8,128)(2,1)S(1)}, bf16[128,1024]{1,0:T(8,128)(2,1)S(1)}, u32[]{:S(2)}, u32[]{:S(2)}) collective-permute-start(bf16[128,1024]{1,0:T(8,128)(2,1)S(1)} %norm.1.refs_0_), channel_id=1, source_target_pairs={{0,128},{64,192},{128,0},{192,64},{1,129},{65,193},{129,1},{193,65... | collective-permute-start | bytes 786440 | tf_op jit(solution)/shard_map/ppermute | solution.py:33
  9.9 8.5 %all-to-all-start = ((bf16[8,64,512]{2,1,0:T(8,128)(2,1)}), bf16[8,64,512]{2,1,0:T(8,128)(2,1)S(1)}, u32[]{:S(2)}, u32[]{:S(2)}) async-start(bf16[8,64,512]{2,1,0:T(8,128)(2,1)} %broadcast_in_dim.18), calls=%async_computation | async-start | bytes 1048576 | tf_op jit(solution)/shard_map/all_to_all | solution.py:48
  18.5 2.1 %collective-permute-start.10 = (bf16[1032,256]{1,0:T(8,128)(2,1)S(1)}, bf16[1032,256]{1,0:T(8,128)(2,1)S(1)}, u32[]{:S(2)}, u32[]{:S(2)}) collective-permute-start(bf16[1032,256]{1,0:T(8,128)(2,1)S(1)} %pad_maximum_fusion.refs_5_.refs_6_), channel_id=1, source_target_pairs={{0,32},{16,51},{32,1},{48,16},{1,33},{17,48},{33,2},{49,17},{2,34}... | collective-permute-start | bytes 1585160 | tf_op jit(solution)/shard_map/ppermute | solution.py:44
  26.8 11.9 %collective-permute-done.10.refs_7_ = bf16[1032,256]{1,0:T(8,128)(2,1)S(1)} collective-permute-done((bf16[1032,256]{1,0:T(8,128)(2,1)S(1)}, bf16[1032,256]{1,0:T(8,128)(2,1)S(1)}, u32[]{:S(2)}, u32[]{:S(2)}) %collective-permute-start.10) | collective-permute-done | bytes 528416 | tf_op jit(solution)/shard_map/ppermute | solution.py:44
  38.7 9.5 %collective-permute-done.21.refs_0_ = bf16[128,1024]{1,0:T(8,128)(2,1)} collective-permute-done((bf16[128,1024]{1,0:T(8,128)(2,1)S(1)}, bf16[128,1024]{1,0:T(8,128)(2,1)}, u32[]{:S(2)}, u32[]{:S(2)}) %collective-permute-start.21) | collective-permute-done | bytes 262176 | tf_op jit(solution)/shard_map/ppermute | solution.py:37
  49.7 3.0 %collective-permute-start.17 = (bf16[1032,256]{1,0:T(8,128)(2,1)S(1)}, bf16[1032,256]{1,0:T(8,128)(2,1)S(1)}, u32[]{:S(2)}, u32[]{:S(2)}) collective-permute-start(bf16[1032,256]{1,0:T(8,128)(2,1)S(1)} %collective-permute-done.11.refs_8_), channel_id=1, source_target_pairs={{0,16},{16,0},{1,17},{17,1},{2,18},{18,2},{3,19},{19,3},{4,20},{20... | collective-permute-start | bytes 1585160 | tf_op jit(solution)/shard_map/ppermute | solution.py:56
  52.7 5.9 %collective-permute-done.6.refs_2_ = bf16[8,64,512]{2,1,0:T(8,128)(2,1)S(1)} collective-permute-done((bf16[8,64,512]{2,1,0:T(8,128)(2,1)S(1)}, bf16[8,64,512]{2,1,0:T(8,128)(2,1)S(1)}, u32[]{:S(2)}, u32[]{:S(2)}) %collective-permute-start.6) | collective-permute-done | bytes 524320 | tf_op jit(solution)/shard_map/ppermute | solution.py:52
  63.2 5.8 %collective-permute-done.7.refs_1_ = bf16[8,64,512]{2,1,0:T(8,128)(2,1)S(1)} collective-permute-done((bf16[8,64,512]{2,1,0:T(8,128)(2,1)S(1)}, bf16[8,64,512]{2,1,0:T(8,128)(2,1)S(1)}, u32[]{:S(2)}, u32[]{:S(2)}) %collective-permute-start.7) | collective-permute-done | bytes 524320 | tf_op jit(solution)/shard_map/ppermute | solution.py:52
  69.0 5.6 %collective-permute-done.4.refs_3_ = bf16[8,64,512]{2,1,0:T(8,128)(2,1)S(1)} collective-permute-done((bf16[8,64,512]{2,1,0:T(8,128)(2,1)S(1)}, bf16[8,64,512]{2,1,0:T(8,128)(2,1)S(1)}, u32[]{:S(2)}, u32[]{:S(2)}) %collective-permute-start.4) | collective-permute-done | bytes 524320 | tf_op jit(solution)/shard_map/ppermute | solution.py:52
  78.7 10.4 %collective-permute-done.23.refs_0_ = bf16[256,1024]{1,0:T(8,128)(2,1)S(1)} collective-permute-done((bf16[256,1024]{1,0:T(8,128)(2,1)S(1)}, bf16[256,1024]{1,0:T(8,128)(2,1)S(1)}, u32[]{:S(2)}, u32[]{:S(2)}) %collective-permute-start.23) | collective-permute-done | bytes 524320 | tf_op jit(solution)/shard_map/ppermute | solution.py:37
  90.1 5.2 %mlp.6 = (bf16[2,512,256]{2,1,0:T(8,128)(2,1)S(1)}, bf16[2,512,256]{2,1,0:T(8,128)(2,1)S(1)}) custom-call(bf16[256,1024]{1,0:T(8,128)(2,1)S(1)} %collective-permute-done.23.refs_0_, bf16[256,1024]{1,0:T(8,128)(2,1)S(1)} %collective-permute-done.24.refs_1_, bf16[4,1024,512]{2,1,0:T(8,128)(2,1)S(1)} %get-tuple-element.28.refs_2_, ...), custom_call_target="tpu_custom_call" | custom-call | flops 100000000 | bytes 8388608 | tf_op jit(solution)/shard_map/mlp/pallas_call | solution.py:228
  96.1 2.0 %collective-permute-start.25 = (bf16[2,512,256]{2,1,0:T(8,128)(2,1)S(1)}, bf16[2,512,256]{2,1,0:T(8,128)(2,1)S(1)}, u32[]{:S(2)}, u32[]{:S(2)}) collective-permute-start(bf16[2,512,256]{2,1,0:T(8,128)(2,1)S(1)} %get-tuple-element.34), channel_id=1, source_target_pairs={{0,4},{4,8},{8,12},{12,0},{1,5},{5,9},{9,13},{13,1},{2,6},{6,10},{... | collective-permute-start | bytes 1572872 | tf_op jit(solution)/shard_map/ppermute | solution.py:37
  98.1 6.4 %mlp.7 = (bf16[2,512,256]{2,1,0:T(8,128)(2,1)S(1)}, bf16[2,512,256]{2,1,0:T(8,128)(2,1)S(1)}) custom-call(bf16[128,1024]{1,0:T(8,128)(2,1)} %collective-permute-done.21.refs_0_, bf16[384,1024]{1,0:T(8,128)(2,1)} %collective-permute-done.22.refs_1_, bf16[4,1024,512]{2,1,0:T(8,128)(2,1)S(1)} %get-tuple-element.28.refs_2_, ...), custom_call_target="tpu_custom_call" | custom-call | flops 100000000 | bytes 8388608 | tf_op jit(solution)/shard_map/mlp/pallas_call | solution.py:228
  104.9 6.1 %mlp.5 = (bf16[2,512,256]{2,1,0:T(8,128)(2,1)S(1)}, bf16[2,512,256]{2,1,0:T(8,128)(2,1)S(1)}) custom-call(bf16[128,1024]{1,0:T(8,128)(2,1)} %collective-permute-done.19.refs_0_, bf16[384,1024]{1,0:T(8,128)(2,1)S(1)} %collective-permute-done.20.refs_1_, bf16[4,1024,512]{2,1,0:T(8,128)(2,1)S(1)} %get-tuple-element.28.refs_2_, ...), custom_call_target="tpu_custom_call" | custom-call | flops 100000000 | bytes 8388608 | tf_op jit(solution)/shard_map/mlp/pallas_call | solution.py:228
  111.0 3.2 %collective-permute-start.28 = (bf16[2,512,256]{2,1,0:T(8,128)(2,1)S(1)}, bf16[2,512,256]{2,1,0:T(8,128)(2,1)S(1)}, u32[]{:S(2)}, u32[]{:S(2)}) collective-permute-start(bf16[2,512,256]{2,1,0:T(8,128)(2,1)S(1)} %get-tuple-element.36), channel_id=1, source_target_pairs={{0,4},{4,8},{8,12},{12,0},{1,5},{5,9},{9,13},{13,1},{2,6},{6,10},{... | collective-permute-start | bytes 1572872 | tf_op jit(solution)/shard_map/ppermute | solution.py:37
  114.5 3.3 %collective-permute-start.34 = (bf16[512,256]{1,0:T(8,128)(2,1)S(1)}, bf16[512,256]{1,0:T(8,128)(2,1)S(1)}, u32[]{:S(2)}, u32[]{:S(2)}) collective-permute-start(bf16[512,256]{1,0:T(8,128)(2,1)S(1)} %add_in.6), channel_id=1, source_target_pairs={{0,4},{4,8},{8,12},{12,0},{1,5},{5,9},{9,13},{13,1},{2,6},{6,10},{... | collective-permute-start | bytes 786440 | tf_op jit(solution)/shard_map/ppermute | solution.py:37
  118.1 4.0 %collective-permute-done.27.one0 = bf16[2,512,256]{2,1,0:T(8,128)(2,1)S(1)} collective-permute-done((bf16[2,512,256]{2,1,0:T(8,128)(2,1)S(1)}, bf16[2,512,256]{2,1,0:T(8,128)(2,1)S(1)}, u32[]{:S(2)}, u32[]{:S(2)}) %collective-permute-start.27) | collective-permute-done | bytes 524320 | tf_op jit(solution)/shard_map/ppermute | solution.py:37
  122.1 3.2 %collective-permute-start.26 = (bf16[512,256]{1,0:T(8,128)(2,1)S(1)}, bf16[512,256]{1,0:T(8,128)(2,1)S(1)}, u32[]{:S(2)}, u32[]{:S(2)}) collective-permute-start(bf16[512,256]{1,0:T(8,128)(2,1)S(1)} %add_in.4), channel_id=1, source_target_pairs={{0,4},{4,8},{8,12},{12,0},{1,5},{5,9},{9,13},{13,1},{2,6},{6,10},{... | collective-permute-start | bytes 786440 | tf_op jit(solution)/shard_map/ppermute | solution.py:37
  125.3 8.6 %mlp.4 = (bf16[2,512,256]{2,1,0:T(8,128)(2,1)S(1)}, bf16[2,512,256]{2,1,0:T(8,128)(2,1)S(1)}) custom-call(bf16[128,1024]{1,0:T(8,128)(2,1)S(1)} %norm.1.refs_0_, bf16[384,1024]{1,0:T(8,128)(2,1)} %constant_dynamic-update-slice_fusion.refs_1_, bf16[4,1024,512]{2,1,0:T(8,128)(2,1)S(1)} %get-tuple-element.28.refs_2_, f32[4,512]{1,0:T(4,128)S(1)} %get-tuple-element.29.refs_3_, ...), custom_call_target="tpu_custom_call" | custom-call | flops 100000000 | bytes 8388608 | tf_op jit(solution)/shard_map/mlp/pallas_call | solution.py:228
  134.3 3.2 %collective-permute-start.37 = (bf16[2,128,256]{2,1,0:T(8,128)(2,1)S(1)}, bf16[2,128,256]{2,1,0:T(8,128)(2,1)S(1)}, u32[]{:S(2)}, u32[]{:S(2)}) collective-permute-start(bf16[2,128,256]{2,1,0:T(8,128)(2,1)S(1)} %get-tuple-element.45), channel_id=1, source_target_pairs={{0,192},{64,0},{128,64},{192,128},{1,193},{65,1},{129,65},{193,129... | collective-permute-start | bytes 393224 | tf_op jit(solution)/shard_map/ppermute | solution.py:33
  138.7 2.4 %collective-permute-start.32 = (bf16[2,128,256]{2,1,0:T(8,128)(2,1)S(1)}, bf16[2,128,256]{2,1,0:T(8,128)(2,1)S(1)}, u32[]{:S(2)}, u32[]{:S(2)}) collective-permute-start(bf16[2,128,256]{2,1,0:T(8,128)(2,1)S(1)} %get-tuple-element.41), channel_id=1, source_target_pairs={{0,192},{64,0},{128,64},{192,128},{1,193},{65,1},{129,65},{193,129... | collective-permute-start | bytes 393224 | tf_op jit(solution)/shard_map/ppermute | solution.py:33
  141.1 3.8 %collective-permute-done.36.refs_5_ = bf16[2,128,256]{2,1,0:T(8,128)(2,1)S(1)} collective-permute-done((bf16[2,128,256]{2,1,0:T(8,128)(2,1)S(1)}, bf16[2,128,256]{2,1,0:T(8,128)(2,1)S(1)}, u32[]{:S(2)}, u32[]{:S(2)}) %collective-permute-start.36) | collective-permute-done | bytes 131104 | tf_op jit(solution)/shard_map/ppermute | solution.py:33
  146.3 5.1 %collective-permute-done.33.refs_3_ = bf16[2,128,256]{2,1,0:T(8,128)(2,1)S(1)} collective-permute-done((bf16[2,128,256]{2,1,0:T(8,128)(2,1)S(1)}, bf16[2,128,256]{2,1,0:T(8,128)(2,1)S(1)}, u32[]{:S(2)}, u32[]{:S(2)}) %collective-permute-start.33) | collective-permute-done | bytes 131104 | tf_op jit(solution)/shard_map/ppermute | solution.py:33
  (95 shorter events, 29.3 us)
Async XLA Ops:
  0.0 18.4 %collective-permute-start.9 = (bf16[512,256]{1,0:T(8,128)(2,1)}, bf16[512,256]{1,0:T(8,128)(2,1)S(1)}, u32[]{:S(2)}, u32[]{:S(2)}) collective-permute-start(bf16[512,256]{1,0:T(8,128)(2,1)} %param.12), channel_id=1, source_target_pairs={{0,16},{16,0},{1,17},{17,1},{2,18},{18,2},{3,19},{19,3},{4,20},{20... | collective-permute-start | bytes 786440 | tf_op jit(solution)/shard_map/ppermute | solution.py:56
  3.1 17.5 %collective-permute-start = (bf16[128,1024]{1,0:T(8,128)(2,1)S(1)}, bf16[128,1024]{1,0:T(8,128)(2,1)S(1)}, u32[]{:S(2)}, u32[]{:S(2)}) collective-permute-start(bf16[128,1024]{1,0:T(8,128)(2,1)S(1)} %norm.1.refs_0_), channel_id=1, source_target_pairs={{0,64},{64,128},{128,192},{192,0},{1,65},{65,129},{129,193},{193,1... | collective-permute-start | bytes 786440 | tf_op jit(solution)/shard_map/ppermute | solution.py:33
  4.7 16.6 %collective-permute-start.1 = (bf16[128,1024]{1,0:T(8,128)(2,1)S(1)}, bf16[128,1024]{1,0:T(8,128)(2,1)S(1)}, u32[]{:S(2)}, u32[]{:S(2)}) collective-permute-start(bf16[128,1024]{1,0:T(8,128)(2,1)S(1)} %norm.1.refs_0_), channel_id=1, source_target_pairs={{0,192},{64,0},{128,64},{192,128},{1,193},{65,1},{129,65},{193,129... | collective-permute-start | bytes 786440 | tf_op jit(solution)/shard_map/ppermute | solution.py:33
  6.4 15.6 %collective-permute-start.2 = (bf16[128,1024]{1,0:T(8,128)(2,1)S(1)}, bf16[128,1024]{1,0:T(8,128)(2,1)S(1)}, u32[]{:S(2)}, u32[]{:S(2)}) collective-permute-start(bf16[128,1024]{1,0:T(8,128)(2,1)S(1)} %norm.1.refs_0_), channel_id=1, source_target_pairs={{0,128},{64,192},{128,0},{192,64},{1,129},{65,193},{129,1},{193,65... | collective-permute-start | bytes 786440 | tf_op jit(solution)/shard_map/ppermute | solution.py:33
  9.9 38.2 %all-to-all-start = ((bf16[8,64,512]{2,1,0:T(8,128)(2,1)}), bf16[8,64,512]{2,1,0:T(8,128)(2,1)S(1)}, u32[]{:S(2)}, u32[]{:S(2)}) async-start(bf16[8,64,512]{2,1,0:T(8,128)(2,1)} %broadcast_in_dim.18), calls=%async_computation | async-start | bytes 1048576 | tf_op jit(solution)/shard_map/all_to_all | solution.py:48
  18.5 20.2 %collective-permute-start.10 = (bf16[1032,256]{1,0:T(8,128)(2,1)S(1)}, bf16[1032,256]{1,0:T(8,128)(2,1)S(1)}, u32[]{:S(2)}, u32[]{:S(2)}) collective-permute-start(bf16[1032,256]{1,0:T(8,128)(2,1)S(1)} %pad_maximum_fusion.refs_5_.refs_6_), channel_id=1, source_target_pairs={{0,32},{16,51},{32,1},{48,16},{1,33},{17,48},{33,2},{49,17},{2,34}... | collective-permute-start | bytes 1585160 | tf_op jit(solution)/shard_map/ppermute | solution.py:44
  22.8 26.4 %collective-permute-start.22 = (bf16[384,1024]{1,0:T(8,128)(2,1)}, bf16[384,1024]{1,0:T(8,128)(2,1)}, u32[]{:S(2)}, u32[]{:S(2)}) collective-permute-start(bf16[384,1024]{1,0:T(8,128)(2,1)} %constant_dynamic-update-slice_fusion.refs_1_), channel_id=1, source_target_pairs={{0,4},{4,8},{8,12},{12,0},{1,5},{5,9},{9,13},{13,1},{2,6},{6,10},{... | collective-permute-start | bytes 2359304 | tf_op jit(solution)/shard_map/ppermute | solution.py:37
  24.1 25.7 %collective-permute-start.20 = (bf16[384,1024]{1,0:T(8,128)(2,1)}, bf16[384,1024]{1,0:T(8,128)(2,1)S(1)}, u32[]{:S(2)}, u32[]{:S(2)}) collective-permute-start(bf16[384,1024]{1,0:T(8,128)(2,1)} %constant_dynamic-update-slice_fusion.refs_1_), channel_id=1, source_target_pairs={{0,12},{4,0},{8,4},{12,8},{1,13},{5,1},{9,5},{13,9},{2,14},{6,2},{... | collective-permute-start | bytes 2359304 | tf_op jit(solution)/shard_map/ppermute | solution.py:37
  24.8 23.4 %collective-permute-start.21 = (bf16[128,1024]{1,0:T(8,128)(2,1)S(1)}, bf16[128,1024]{1,0:T(8,128)(2,1)}, u32[]{:S(2)}, u32[]{:S(2)}) collective-permute-start(bf16[128,1024]{1,0:T(8,128)(2,1)S(1)} %norm.1.refs_0_), channel_id=1, source_target_pairs={{0,4},{4,8},{8,12},{12,0},{1,5},{5,9},{9,13},{13,1},{2,6},{6,10},{... | collective-permute-start | bytes 786440 | tf_op jit(solution)/shard_map/ppermute | solution.py:37
  26.1 23.1 %collective-permute-start.19 = (bf16[128,1024]{1,0:T(8,128)(2,1)S(1)}, bf16[128,1024]{1,0:T(8,128)(2,1)}, u32[]{:S(2)}, u32[]{:S(2)}) collective-permute-start(bf16[128,1024]{1,0:T(8,128)(2,1)S(1)} %norm.1.refs_0_), channel_id=1, source_target_pairs={{0,12},{4,0},{8,4},{12,8},{1,13},{5,1},{9,5},{13,9},{2,14},{6,2},{... | collective-permute-start | bytes 786440 | tf_op jit(solution)/shard_map/ppermute | solution.py:37
  58.6 16.0 %collective-permute-start.4 = (bf16[8,64,512]{2,1,0:T(8,128)(2,1)S(1)}, bf16[8,64,512]{2,1,0:T(8,128)(2,1)S(1)}, u32[]{:S(2)}, u32[]{:S(2)}) collective-permute-start(bf16[8,64,512]{2,1,0:T(8,128)(2,1)S(1)} %collective-permute-done.3.refs_1_), channel_id=1, source_target_pairs={{0,64},{16,208},{64,128},{80,16},{128,192},{144,80},{192,0},{208,1... | collective-permute-start | bytes 1572872 | tf_op jit(solution)/shard_map/ppermute | solution.py:52
  59.1 15.6 %collective-permute-start.18 = (bf16[8,64,512]{2,1,0:T(8,128)(2,1)S(1)}, bf16[8,64,512]{2,1,0:T(8,128)(2,1)S(1)}, u32[]{:S(2)}, u32[]{:S(2)}) collective-permute-start(bf16[8,64,512]{2,1,0:T(8,128)(2,1)S(1)} %collective-permute-done.6.refs_2_), channel_id=1, source_target_pairs={{0,16},{16,0},{1,17},{17,1},{2,18},{18,2},{3,19},{19,3},{4,20},{20... | collective-permute-start | bytes 1572872 | tf_op jit(solution)/shard_map/ppermute | solution.py:56
  60.1 16.6 %collective-permute-start.13 = (bf16[1032,256]{1,0:T(8,128)(2,1)S(1)}, bf16[1032,256]{1,0:T(8,128)(2,1)S(1)}, u32[]{:S(2)}, u32[]{:S(2)}) collective-permute-start(bf16[1032,256]{1,0:T(8,128)(2,1)S(1)} %collective-permute-done.12.refs_11_.refs_9_), channel_id=1, source_target_pairs={{0,16},{16,0},{1,17},{17,1},{2,18},{18,2},{3,19},{19,3},{4,20},{20... | collective-permute-start | bytes 1585160 | tf_op jit(solution)/shard_map/ppermute | solution.py:56
  60.2 15.8 %collective-permute-start.14 = (bf16[520,256]{1,0:T(8,128)(2,1)S(1)}, bf16[520,256]{1,0:T(8,128)(2,1)S(1)}, u32[]{:S(2)}, u32[]{:S(2)}) collective-permute-start(bf16[520,256]{1,0:T(8,128)(2,1)S(1)} %slice.20), channel_id=1, source_target_pairs={{0,32},{16,51},{32,1},{48,16},{1,33},{17,48},{33,2},{49,17},{2,34}... | collective-permute-start | bytes 798728 | tf_op jit(solution)/shard_map/ppermute | solution.py:44
  74.6 14.4 %collective-permute-start.23 = (bf16[256,1024]{1,0:T(8,128)(2,1)S(1)}, bf16[256,1024]{1,0:T(8,128)(2,1)S(1)}, u32[]{:S(2)}, u32[]{:S(2)}) collective-permute-start(bf16[256,1024]{1,0:T(8,128)(2,1)S(1)} %pad_maximum_fusion.1), channel_id=1, source_target_pairs={{0,4},{4,8},{8,12},{12,0},{1,5},{5,9},{9,13},{13,1},{2,6},{6,10},{... | collective-permute-start | bytes 1572872 | tf_op jit(solution)/shard_map/ppermute | solution.py:37
  76.0 14.1 %collective-permute-start.24 = (bf16[256,1024]{1,0:T(8,128)(2,1)S(1)}, bf16[256,1024]{1,0:T(8,128)(2,1)S(1)}, u32[]{:S(2)}, u32[]{:S(2)}) collective-permute-start(bf16[256,1024]{1,0:T(8,128)(2,1)S(1)} %pad_maximum_fusion.2), channel_id=1, source_target_pairs={{0,12},{4,0},{8,4},{12,8},{1,13},{5,1},{9,5},{13,9},{2,14},{6,2},{... | collective-permute-start | bytes 1572872 | tf_op jit(solution)/shard_map/ppermute | solution.py:37
  95.3 19.0 %collective-permute-start.29 = (bf16[2,512,256]{2,1,0:T(8,128)(2,1)S(1)}, bf16[2,512,256]{2,1,0:T(8,128)(2,1)S(1)}, u32[]{:S(2)}, u32[]{:S(2)}) collective-permute-start(bf16[2,512,256]{2,1,0:T(8,128)(2,1)S(1)} %get-tuple-element.38), channel_id=1, source_target_pairs={{0,12},{4,0},{8,4},{12,8},{1,13},{5,1},{9,5},{13,9},{2,14},{6,2},{... | collective-permute-start | bytes 1572872 | tf_op jit(solution)/shard_map/ppermute | solution.py:37
  96.1 18.3 %collective-permute-start.25 = (bf16[2,512,256]{2,1,0:T(8,128)(2,1)S(1)}, bf16[2,512,256]{2,1,0:T(8,128)(2,1)S(1)}, u32[]{:S(2)}, u32[]{:S(2)}) collective-permute-start(bf16[2,512,256]{2,1,0:T(8,128)(2,1)S(1)} %get-tuple-element.34), channel_id=1, source_target_pairs={{0,4},{4,8},{8,12},{12,0},{1,5},{5,9},{9,13},{13,1},{2,6},{6,10},{... | collective-permute-start | bytes 1572872 | tf_op jit(solution)/shard_map/ppermute | solution.py:37
  104.6 17.5 %collective-permute-start.27 = (bf16[2,512,256]{2,1,0:T(8,128)(2,1)S(1)}, bf16[2,512,256]{2,1,0:T(8,128)(2,1)S(1)}, u32[]{:S(2)}, u32[]{:S(2)}) collective-permute-start(bf16[2,512,256]{2,1,0:T(8,128)(2,1)S(1)} %get-tuple-element.35), channel_id=1, source_target_pairs={{0,12},{4,0},{8,4},{12,8},{1,13},{5,1},{9,5},{13,9},{2,14},{6,2},{... | collective-permute-start | bytes 1572872 | tf_op jit(solution)/shard_map/ppermute | solution.py:37
  111.0 22.9 %collective-permute-start.28 = (bf16[2,512,256]{2,1,0:T(8,128)(2,1)S(1)}, bf16[2,512,256]{2,1,0:T(8,128)(2,1)S(1)}, u32[]{:S(2)}, u32[]{:S(2)}) collective-permute-start(bf16[2,512,256]{2,1,0:T(8,128)(2,1)S(1)} %get-tuple-element.36), channel_id=1, source_target_pairs={{0,4},{4,8},{8,12},{12,0},{1,5},{5,9},{9,13},{13,1},{2,6},{6,10},{... | collective-permute-start | bytes 1572872 | tf_op jit(solution)/shard_map/ppermute | solution.py:37
  114.3 19.6 %collective-permute-start.35 = (bf16[512,256]{1,0:T(8,128)(2,1)S(1)}, bf16[512,256]{1,0:T(8,128)(2,1)S(1)}, u32[]{:S(2)}, u32[]{:S(2)}) collective-permute-start(bf16[512,256]{1,0:T(8,128)(2,1)S(1)} %add_in.7), channel_id=1, source_target_pairs={{0,12},{4,0},{8,4},{12,8},{1,13},{5,1},{9,5},{13,9},{2,14},{6,2},{... | collective-permute-start | bytes 786440 | tf_op jit(solution)/shard_map/ppermute | solution.py:37
  114.5 19.4 %collective-permute-start.34 = (bf16[512,256]{1,0:T(8,128)(2,1)S(1)}, bf16[512,256]{1,0:T(8,128)(2,1)S(1)}, u32[]{:S(2)}, u32[]{:S(2)}) collective-permute-start(bf16[512,256]{1,0:T(8,128)(2,1)S(1)} %add_in.6), channel_id=1, source_target_pairs={{0,4},{4,8},{8,12},{12,0},{1,5},{5,9},{9,13},{13,1},{2,6},{6,10},{... | collective-permute-start | bytes 786440 | tf_op jit(solution)/shard_map/ppermute | solution.py:37
  117.9 19.6 %collective-permute-start.30 = (bf16[512,256]{1,0:T(8,128)(2,1)S(1)}, bf16[512,256]{1,0:T(8,128)(2,1)S(1)}, u32[]{:S(2)}, u32[]{:S(2)}) collective-permute-start(bf16[512,256]{1,0:T(8,128)(2,1)S(1)} %add_in.5), channel_id=1, source_target_pairs={{0,12},{4,0},{8,4},{12,8},{1,13},{5,1},{9,5},{13,9},{2,14},{6,2},{... | collective-permute-start | bytes 786440 | tf_op jit(solution)/shard_map/ppermute | solution.py:37
  122.1 15.5 %collective-permute-start.26 = (bf16[512,256]{1,0:T(8,128)(2,1)S(1)}, bf16[512,256]{1,0:T(8,128)(2,1)S(1)}, u32[]{:S(2)}, u32[]{:S(2)}) collective-permute-start(bf16[512,256]{1,0:T(8,128)(2,1)S(1)} %add_in.4), channel_id=1, source_target_pairs={{0,4},{4,8},{8,12},{12,0},{1,5},{5,9},{9,13},{13,1},{2,6},{6,10},{... | collective-permute-start | bytes 786440 | tf_op jit(solution)/shard_map/ppermute | solution.py:37
  (22 other events, 188.3 us)
where the time goes:
time: 153 us
  waiting for transfers between devices  66.9 us (44%)
  starting transfers between devices  46.2 us (30%)
  Pallas kernels  29.7 us (19%)
  local copies, waits for them, and re-layouts  9.08 us (6%)
    pallas_call x4, Pallas kernels, mlp(): pl.pallas_call(small_mlp_kernel if small else functools.partial(mlp_kerne...  26.3 us
    ppermute x14, waiting for transfers between devices, on_y(): return lax.ppermute(a, 'y', ring(Y, d))  25.3 us
    ppermute x14, starting transfers between devices, on_y(): return lax.ppermute(a, 'y', ring(Y, d))  19.2 us
    ppermute x3, waiting for transfers between devices, on_xc(): return lax.ppermute(a, ('x', 'c'), both_ways(X))  17.3 us
    ppermute x4, waiting for transfers between devices, on_z(): lax.ppermute(a, ('zl', 'c', 'zh'), [(at(i), at(j)) for i, j in both_ways(...  13 us
    ppermute x9, starting transfers between devices, on_x(): return lax.ppermute(a, 'x', ring(X, d))  11.8 us
    ppermute x9, waiting for transfers between devices, on_x(): return lax.ppermute(a, 'x', ring(X, d))  10.3 us
    all_to_all x1, starting transfers between devices, over_z(): lax.all_to_all(a, ('zl', 'zh'), split_axis=0, concat_axis=0, tiled=True)  8.47 us
  transfers between devices with their start and end apart: 40, of which 14 were waited for; matrix products, arithmetic and copies ran while one was open for 4% of the time, Pallas kernels for 15%

commit v1 on v0

--- a/solution.py
+++ b/solution.py
@@ -77,6 +77,24 @@
         name="norm",
         cost_estimate=pl.CostEstimate(flops=10**6, bytes_accessed=2**19, transcendentals=128),
     )(rows, gain[None], bias[None])
+
+
+def copies_kernel(w_ref, o_ref):
+    @pl.loop(0, Z)
+    def _(i):
+        o_ref[i] = w_ref[...]
+
+
+def copies_of(w):
+    return pl.pallas_call(
+        copies_kernel,
+        out_shape=jax.ShapeDtypeStruct((Z, *w.shape), BF),
+        in_specs=[VMEM],
+        out_specs=VMEM,
+        compiler_params=pltpu.CompilerParams(vmem_limit_bytes=2 * 2**20),
+        name="copies",
+        cost_estimate=pl.CostEstimate(flops=10**5, bytes_accessed=2**19, transcendentals=0),
+    )(w)
 
 
 def side(c):
@@ -180,13 +198,17 @@
     )(b[None])
 
 
+def fill(t_ref, toks, plan):
+    for t, parts in zip(toks, plan):
+        for src, dst, n in parts:
+            t_ref[dst : dst + n] = t[src : src + n]
+
+
 def mlp_kernel(plan, *refs):
     toks, (up, bias, down), outs, (t_ref, h_ref) = (
         refs[:-7], refs[-7:-4], refs[-4:-2], refs[-2:],
     )
-    for t, parts in zip(toks, plan):
-        for src, dst, n in parts:
-            t_ref[dst : dst + n] = t[src : src + n]
+    fill(t_ref, toks, plan)
 
     @pl.loop(0, 2)
     def _(i):
@@ -199,12 +221,11 @@
             outs[j % 2][j // 2, rows] = o.astype(BF)
 
 
-def small_mlp_kernel(*refs):
+def short_mlp_kernel(plan, *refs):
     toks, (up, bias, down), outs, (t_ref, h_ref) = (
         refs[:-7], refs[-7:-4], refs[-4:-2], refs[-2:],
     )
-    t_ref[0:128] = toks[0][...]
-    t_ref[128:512] = toks[1][...]
+    fill(t_ref, toks, plan)
 
     @pl.loop(0, 2)
     def _(i):
@@ -222,19 +243,18 @@
                 outs[j][h, rows] = o.astype(BF)
 
 
-def mlp(toks, plan, up, bias, down, small=False):
-    rows = 512
-    half = jax.ShapeDtypeStruct((2, rows, COLS), BF)
-    return pl.pallas_call(
-        small_mlp_kernel if small else functools.partial(mlp_kernel, plan),
+def mlp(toks, plan, up, bias, down, kernel=mlp_kernel):
+    half = jax.ShapeDtypeStruct((2, 512, COLS), BF)
+    return pl.pallas_call(
+        functools.partial(kernel, plan),
         out_shape=(half, half),
         in_specs=[VMEM] * (len(toks) + 3),
         out_specs=(VMEM, VMEM),
-        scratch_shapes=[pltpu.VMEM((rows, D), BF), pltpu.VMEM((256, HID), BF)],
+        scratch_shapes=[pltpu.VMEM((512, D), BF), pltpu.VMEM((256, HID), BF)],
         compiler_params=pltpu.CompilerParams(vmem_limit_bytes=20 * 2**20),
         name="mlp",
         cost_estimate=pl.CostEstimate(
-            flops=10**8, bytes_accessed=2**23, transcendentals=rows * HID
+            flops=10**8, bytes_accessed=2**23, transcendentals=512 * HID
         ),
     )(*toks, up, bias, down)
 
@@ -324,8 +344,7 @@
     half1 = jnp.concatenate([above[0][64:], above[1][192:]], axis=0)
     far = [on_y(half0, 1), on_y(half1, -1)]
 
-    copies = jnp.broadcast_to(up_weight, (Z, *up_weight.shape))
-    f = over_z(copies)
+    f = over_z(copies_of(up_weight))
     g = on_c(f)
     x1f, x1g = on_xc(f), on_xc(g)
     x2f = on_xc(x1f)
@@ -345,13 +364,13 @@
     up, down, bias = place(UP_LATE, DOWN_LATE, BIASES, pieces, early)
     halves = (((0, 0, 64), (64, 128, 192)), ((0, 64, 64), (64, 320, 192)))
     wholes = (((0, 0, 128),), ((0, 128, 384),))
+    above0, above1 = mlp(above, wholes, up, bias, down)
+    one1 = on_y(above1, 1)
     far0, far1 = mlp(far, halves, up, bias, down)
     from_below, from_above = on_y(far0, 1), on_y(far1, -1)
-    above0, above1 = mlp(above, wholes, up, bias, down)
-    one1 = on_y(above1, 1)
     below0, below1 = mlp(below, wholes, up, bias, down)
     one0 = on_y(below0, -1)
-    own0, own1 = mlp([own, rest], wholes, up, bias, down, True)
+    own0, own1 = mlp([own, rest], wholes, up, bias, down, short_mlp_kernel)
     placed = []
     for h in range(2):
         sum0 = on_y(add_in(above0, from_below, h), 1)

time: 153 us -> 153 us (level)
    broadcast_in_dim x1 -> x0, local copies, waits for them, and re-layouts: 1.68 us -> none  [step(): copies = jnp.broadcast_to(up_weight, (Z, *up_weight.shape))]
    pallas_call x4 -> x5, Pallas kernels: 26.3 us -> 27.2 us  [the longest x4 26.3 us: mlp(): pl.pallas_call(functools.partial(kernel, plan), out_shape=(half, half), i...]
    unnamed x14 -> x16, local copies, waits for them, and re-layouts: 3.78 us -> 4.62 us
  transfers between devices with their start and end apart: 40 -> 40, of which waited for: 14 -> 14; matrix products, arithmetic and copies ran while one was open for 4% -> 3% of each run, Pallas kernels for 15% -> 16%
where the time goes in v1:
time: 153 us
  waiting for transfers between devices  66.9 us (44%)
  starting transfers between devices  46.2 us (30%)
  Pallas kernels  30.6 us (20%)
  local copies, waits for them, and re-layouts  8.24 us (5%)
    pallas_call x4, Pallas kernels, mlp(): pl.pallas_call(functools.partial(kernel, plan), out_shape=(half, half), i...  26.3 us
    ppermute x14, waiting for transfers between devices, on_y(): return lax.ppermute(a, 'y', ring(Y, d))  25.3 us
    ppermute x14, starting transfers between devices, on_y(): return lax.ppermute(a, 'y', ring(Y, d))  19.2 us
    ppermute x3, waiting for transfers between devices, on_xc(): return lax.ppermute(a, ('x', 'c'), both_ways(X))  17.3 us
    ppermute x4, waiting for transfers between devices, on_z(): lax.ppermute(a, ('zl', 'c', 'zh'), [(at(i), at(j)) for i, j in both_ways(...  13 us
    ppermute x9, starting transfers between devices, on_x(): return lax.ppermute(a, 'x', ring(X, d))  11.8 us
    ppermute x9, waiting for transfers between devices, on_x(): return lax.ppermute(a, 'x', ring(X, d))  10.3 us
    all_to_all x1, starting transfers between devices, over_z(): lax.all_to_all(a, ('zl', 'zh'), split_axis=0, concat_axis=0, tiled=True)  8.47 us
  transfers between devices with their start and end apart: 40, of which 14 were waited for; matrix products, arithmetic and copies ran while one was open for 3% of the time, Pallas kernels for 16%

profile of v1, /device:TPU:16, one launch (start us, length us, event | category | flops | bytes accessed | tf_op | source)
XLA Modules:
  0.0 152.5 jit_solution(2393679631122264482)
XLA Ops:
  4.7 1.7 %collective-permute-start.1 = (bf16[128,1024]{1,0:T(8,128)(2,1)S(1)}, bf16[128,1024]{1,0:T(8,128)(2,1)S(1)}, u32[]{:S(2)}, u32[]{:S(2)}) collective-permute-start(bf16[128,1024]{1,0:T(8,128)(2,1)S(1)} %norm.1.refs_0_), channel_id=1, source_target_pairs={{0,192},{64,0},{128,64},{192,128},{1,193},{65,1},{129,65},{193,129... | collective-permute-start | bytes 786440 | tf_op jit(solution)/shard_map/ppermute | solution.py:33
  6.4 1.8 %collective-permute-start.2 = (bf16[128,1024]{1,0:T(8,128)(2,1)S(1)}, bf16[128,1024]{1,0:T(8,128)(2,1)S(1)}, u32[]{:S(2)}, u32[]{:S(2)}) collective-permute-start(bf16[128,1024]{1,0:T(8,128)(2,1)S(1)} %norm.1.refs_0_), channel_id=1, source_target_pairs={{0,128},{64,192},{128,0},{192,64},{1,129},{65,193},{129,1},{193,65... | collective-permute-start | bytes 786440 | tf_op jit(solution)/shard_map/ppermute | solution.py:33
  9.9 8.5 %all-to-all-start = ((bf16[8,64,512]{2,1,0:T(8,128)(2,1)}), bf16[8,64,512]{2,1,0:T(8,128)(2,1)S(1)}, u32[]{:S(2)}, u32[]{:S(2)}) async-start(bf16[8,64,512]{2,1,0:T(8,128)(2,1)} %copies.1), calls=%async_computation | async-start | bytes 1048576 | tf_op jit(solution)/shard_map/all_to_all | solution.py:48
  18.5 2.1 %collective-permute-start.10 = (bf16[1032,256]{1,0:T(8,128)(2,1)S(1)}, bf16[1032,256]{1,0:T(8,128)(2,1)S(1)}, u32[]{:S(2)}, u32[]{:S(2)}) collective-permute-start(bf16[1032,256]{1,0:T(8,128)(2,1)S(1)} %pad_maximum_fusion.refs_5_.refs_6_), channel_id=1, source_target_pairs={{0,32},{16,51},{32,1},{48,16},{1,33},{17,48},{33,2},{49,17},{2,34}... | collective-permute-start | bytes 1585160 | tf_op jit(solution)/shard_map/ppermute | solution.py:44
  26.8 11.9 %collective-permute-done.10.refs_7_ = bf16[1032,256]{1,0:T(8,128)(2,1)S(1)} collective-permute-done((bf16[1032,256]{1,0:T(8,128)(2,1)S(1)}, bf16[1032,256]{1,0:T(8,128)(2,1)S(1)}, u32[]{:S(2)}, u32[]{:S(2)}) %collective-permute-start.10) | collective-permute-done | bytes 528416 | tf_op jit(solution)/shard_map/ppermute | solution.py:44
  38.7 9.5 %collective-permute-done.21.refs_0_ = bf16[128,1024]{1,0:T(8,128)(2,1)} collective-permute-done((bf16[128,1024]{1,0:T(8,128)(2,1)S(1)}, bf16[128,1024]{1,0:T(8,128)(2,1)}, u32[]{:S(2)}, u32[]{:S(2)}) %collective-permute-start.21) | collective-permute-done | bytes 262176 | tf_op jit(solution)/shard_map/ppermute | solution.py:37
  49.7 3.0 %collective-permute-start.17 = (bf16[1032,256]{1,0:T(8,128)(2,1)S(1)}, bf16[1032,256]{1,0:T(8,128)(2,1)S(1)}, u32[]{:S(2)}, u32[]{:S(2)}) collective-permute-start(bf16[1032,256]{1,0:T(8,128)(2,1)S(1)} %collective-permute-done.11.refs_8_), channel_id=1, source_target_pairs={{0,16},{16,0},{1,17},{17,1},{2,18},{18,2},{3,19},{19,3},{4,20},{20... | collective-permute-start | bytes 1585160 | tf_op jit(solution)/shard_map/ppermute | solution.py:56
  52.7 5.9 %collective-permute-done.6.refs_2_ = bf16[8,64,512]{2,1,0:T(8,128)(2,1)S(1)} collective-permute-done((bf16[8,64,512]{2,1,0:T(8,128)(2,1)S(1)}, bf16[8,64,512]{2,1,0:T(8,128)(2,1)S(1)}, u32[]{:S(2)}, u32[]{:S(2)}) %collective-permute-start.6) | collective-permute-done | bytes 524320 | tf_op jit(solution)/shard_map/ppermute | solution.py:52
  63.2 5.8 %collective-permute-done.7.refs_1_ = bf16[8,64,512]{2,1,0:T(8,128)(2,1)S(1)} collective-permute-done((bf16[8,64,512]{2,1,0:T(8,128)(2,1)S(1)}, bf16[8,64,512]{2,1,0:T(8,128)(2,1)S(1)}, u32[]{:S(2)}, u32[]{:S(2)}) %collective-permute-start.7) | collective-permute-done | bytes 524320 | tf_op jit(solution)/shard_map/ppermute | solution.py:52
  69.0 5.6 %collective-permute-done.4.refs_3_ = bf16[8,64,512]{2,1,0:T(8,128)(2,1)S(1)} collective-permute-done((bf16[8,64,512]{2,1,0:T(8,128)(2,1)S(1)}, bf16[8,64,512]{2,1,0:T(8,128)(2,1)S(1)}, u32[]{:S(2)}, u32[]{:S(2)}) %collective-permute-start.4) | collective-permute-done | bytes 524320 | tf_op jit(solution)/shard_map/ppermute | solution.py:52
  78.7 10.4 %collective-permute-done.23.refs_0_ = bf16[256,1024]{1,0:T(8,128)(2,1)S(1)} collective-permute-done((bf16[256,1024]{1,0:T(8,128)(2,1)S(1)}, bf16[256,1024]{1,0:T(8,128)(2,1)S(1)}, u32[]{:S(2)}, u32[]{:S(2)}) %collective-permute-start.23) | collective-permute-done | bytes 524320 | tf_op jit(solution)/shard_map/ppermute | solution.py:37
  90.1 5.2 %mlp.6 = (bf16[2,512,256]{2,1,0:T(8,128)(2,1)S(1)}, bf16[2,512,256]{2,1,0:T(8,128)(2,1)S(1)}) custom-call(bf16[256,1024]{1,0:T(8,128)(2,1)S(1)} %collective-permute-done.23.refs_0_, bf16[256,1024]{1,0:T(8,128)(2,1)S(1)} %collective-permute-done.24.refs_1_, bf16[4,1024,512]{2,1,0:T(8,128)(2,1)S(1)} %get-tuple-element.28.refs_2_, ...), custom_call_target="tpu_custom_call" | custom-call | flops 100000000 | bytes 8388608 | tf_op jit(solution)/shard_map/mlp/pallas_call | solution.py:248
  96.1 2.0 %collective-permute-start.25 = (bf16[2,512,256]{2,1,0:T(8,128)(2,1)S(1)}, bf16[2,512,256]{2,1,0:T(8,128)(2,1)S(1)}, u32[]{:S(2)}, u32[]{:S(2)}) collective-permute-start(bf16[2,512,256]{2,1,0:T(8,128)(2,1)S(1)} %get-tuple-element.34), channel_id=1, source_target_pairs={{0,4},{4,8},{8,12},{12,0},{1,5},{5,9},{9,13},{13,1},{2,6},{6,10},{... | collective-permute-start | bytes 1572872 | tf_op jit(solution)/shard_map/ppermute | solution.py:37
  98.1 6.4 %mlp.7 = (bf16[2,512,256]{2,1,0:T(8,128)(2,1)S(1)}, bf16[2,512,256]{2,1,0:T(8,128)(2,1)S(1)}) custom-call(bf16[128,1024]{1,0:T(8,128)(2,1)} %collective-permute-done.21.refs_0_, bf16[384,1024]{1,0:T(8,128)(2,1)} %collective-permute-done.22.refs_1_, bf16[4,1024,512]{2,1,0:T(8,128)(2,1)S(1)} %get-tuple-element.28.refs_2_, ...), custom_call_target="tpu_custom_call" | custom-call | flops 100000000 | bytes 8388608 | tf_op jit(solution)/shard_map/mlp/pallas_call | solution.py:248
  104.9 6.1 %mlp.5 = (bf16[2,512,256]{2,1,0:T(8,128)(2,1)S(1)}, bf16[2,512,256]{2,1,0:T(8,128)(2,1)S(1)}) custom-call(bf16[128,1024]{1,0:T(8,128)(2,1)} %collective-permute-done.19.refs_0_, bf16[384,1024]{1,0:T(8,128)(2,1)S(1)} %collective-permute-done.20.refs_1_, bf16[4,1024,512]{2,1,0:T(8,128)(2,1)S(1)} %get-tuple-element.28.refs_2_, ...), custom_call_target="tpu_custom_call" | custom-call | flops 100000000 | bytes 8388608 | tf_op jit(solution)/shard_map/mlp/pallas_call | solution.py:248
  111.0 3.2 %collective-permute-start.28 = (bf16[2,512,256]{2,1,0:T(8,128)(2,1)S(1)}, bf16[2,512,256]{2,1,0:T(8,128)(2,1)S(1)}, u32[]{:S(2)}, u32[]{:S(2)}) collective-permute-start(bf16[2,512,256]{2,1,0:T(8,128)(2,1)S(1)} %get-tuple-element.36), channel_id=1, source_target_pairs={{0,4},{4,8},{8,12},{12,0},{1,5},{5,9},{9,13},{13,1},{2,6},{6,10},{... | collective-permute-start | bytes 1572872 | tf_op jit(solution)/shard_map/ppermute | solution.py:37
  114.5 3.3 %collective-permute-start.34 = (bf16[512,256]{1,0:T(8,128)(2,1)S(1)}, bf16[512,256]{1,0:T(8,128)(2,1)S(1)}, u32[]{:S(2)}, u32[]{:S(2)}) collective-permute-start(bf16[512,256]{1,0:T(8,128)(2,1)S(1)} %add_in.6), channel_id=1, source_target_pairs={{0,4},{4,8},{8,12},{12,0},{1,5},{5,9},{9,13},{13,1},{2,6},{6,10},{... | collective-permute-start | bytes 786440 | tf_op jit(solution)/shard_map/ppermute | solution.py:37
  118.1 4.0 %collective-permute-done.27.one0 = bf16[2,512,256]{2,1,0:T(8,128)(2,1)S(1)} collective-permute-done((bf16[2,512,256]{2,1,0:T(8,128)(2,1)S(1)}, bf16[2,512,256]{2,1,0:T(8,128)(2,1)S(1)}, u32[]{:S(2)}, u32[]{:S(2)}) %collective-permute-start.27) | collective-permute-done | bytes 524320 | tf_op jit(solution)/shard_map/ppermute | solution.py:37
  122.1 3.2 %collective-permute-start.26 = (bf16[512,256]{1,0:T(8,128)(2,1)S(1)}, bf16[512,256]{1,0:T(8,128)(2,1)S(1)}, u32[]{:S(2)}, u32[]{:S(2)}) collective-permute-start(bf16[512,256]{1,0:T(8,128)(2,1)S(1)} %add_in.4), channel_id=1, source_target_pairs={{0,4},{4,8},{8,12},{12,0},{1,5},{5,9},{9,13},{13,1},{2,6},{6,10},{... | collective-permute-start | bytes 786440 | tf_op jit(solution)/shard_map/ppermute | solution.py:37
  125.3 8.6 %mlp.4 = (bf16[2,512,256]{2,1,0:T(8,128)(2,1)S(1)}, bf16[2,512,256]{2,1,0:T(8,128)(2,1)S(1)}) custom-call(bf16[128,1024]{1,0:T(8,128)(2,1)S(1)} %norm.1.refs_0_, bf16[384,1024]{1,0:T(8,128)(2,1)} %constant_dynamic-update-slice_fusion.refs_1_, bf16[4,1024,512]{2,1,0:T(8,128)(2,1)S(1)} %get-tuple-element.28.refs_2_, f32[4,512]{1,0:T(4,128)S(1)} %get-tuple-element.29.refs_3_, ...), custom_call_target="tpu_custom_call" | custom-call | flops 100000000 | bytes 8388608 | tf_op jit(solution)/shard_map/mlp/pallas_call | solution.py:248
  134.3 3.2 %collective-permute-start.37 = (bf16[2,128,256]{2,1,0:T(8,128)(2,1)S(1)}, bf16[2,128,256]{2,1,0:T(8,128)(2,1)S(1)}, u32[]{:S(2)}, u32[]{:S(2)}) collective-permute-start(bf16[2,128,256]{2,1,0:T(8,128)(2,1)S(1)} %get-tuple-element.45), channel_id=1, source_target_pairs={{0,192},{64,0},{128,64},{192,128},{1,193},{65,1},{129,65},{193,129... | collective-permute-start | bytes 393224 | tf_op jit(solution)/shard_map/ppermute | solution.py:33
  138.7 2.4 %collective-permute-start.32 = (bf16[2,128,256]{2,1,0:T(8,128)(2,1)S(1)}, bf16[2,128,256]{2,1,0:T(8,128)(2,1)S(1)}, u32[]{:S(2)}, u32[]{:S(2)}) collective-permute-start(bf16[2,128,256]{2,1,0:T(8,128)(2,1)S(1)} %get-tuple-element.41), channel_id=1, source_target_pairs={{0,192},{64,0},{128,64},{192,128},{1,193},{65,1},{129,65},{193,129... | collective-permute-start | bytes 393224 | tf_op jit(solution)/shard_map/ppermute | solution.py:33
  141.1 3.8 %collective-permute-done.36.refs_5_ = bf16[2,128,256]{2,1,0:T(8,128)(2,1)S(1)} collective-permute-done((bf16[2,128,256]{2,1,0:T(8,128)(2,1)S(1)}, bf16[2,128,256]{2,1,0:T(8,128)(2,1)S(1)}, u32[]{:S(2)}, u32[]{:S(2)}) %collective-permute-start.36) | collective-permute-done | bytes 131104 | tf_op jit(solution)/shard_map/ppermute | solution.py:33
  146.3 5.1 %collective-permute-done.33.refs_3_ = bf16[2,128,256]{2,1,0:T(8,128)(2,1)S(1)} collective-permute-done((bf16[2,128,256]{2,1,0:T(8,128)(2,1)S(1)}, bf16[2,128,256]{2,1,0:T(8,128)(2,1)S(1)}, u32[]{:S(2)}, u32[]{:S(2)}) %collective-permute-start.33) | collective-permute-done | bytes 131104 | tf_op jit(solution)/shard_map/ppermute | solution.py:33
  (97 shorter events, 29.3 us)
Async XLA Ops:
  0.0 18.4 %collective-permute-start.9 = (bf16[512,256]{1,0:T(8,128)(2,1)}, bf16[512,256]{1,0:T(8,128)(2,1)S(1)}, u32[]{:S(2)}, u32[]{:S(2)}) collective-permute-start(bf16[512,256]{1,0:T(8,128)(2,1)} %param.12), channel_id=1, source_target_pairs={{0,16},{16,0},{1,17},{17,1},{2,18},{18,2},{3,19},{19,3},{4,20},{20... | collective-permute-start | bytes 786440 | tf_op jit(solution)/shard_map/ppermute | solution.py:56
  3.1 17.5 %collective-permute-start = (bf16[128,1024]{1,0:T(8,128)(2,1)S(1)}, bf16[128,1024]{1,0:T(8,128)(2,1)S(1)}, u32[]{:S(2)}, u32[]{:S(2)}) collective-permute-start(bf16[128,1024]{1,0:T(8,128)(2,1)S(1)} %norm.1.refs_0_), channel_id=1, source_target_pairs={{0,64},{64,128},{128,192},{192,0},{1,65},{65,129},{129,193},{193,1... | collective-permute-start | bytes 786440 | tf_op jit(solution)/shard_map/ppermute | solution.py:33
  4.7 16.6 %collective-permute-start.1 = (bf16[128,1024]{1,0:T(8,128)(2,1)S(1)}, bf16[128,1024]{1,0:T(8,128)(2,1)S(1)}, u32[]{:S(2)}, u32[]{:S(2)}) collective-permute-start(bf16[128,1024]{1,0:T(8,128)(2,1)S(1)} %norm.1.refs_0_), channel_id=1, source_target_pairs={{0,192},{64,0},{128,64},{192,128},{1,193},{65,1},{129,65},{193,129... | collective-permute-start | bytes 786440 | tf_op jit(solution)/shard_map/ppermute | solution.py:33
  6.4 15.6 %collective-permute-start.2 = (bf16[128,1024]{1,0:T(8,128)(2,1)S(1)}, bf16[128,1024]{1,0:T(8,128)(2,1)S(1)}, u32[]{:S(2)}, u32[]{:S(2)}) collective-permute-start(bf16[128,1024]{1,0:T(8,128)(2,1)S(1)} %norm.1.refs_0_), channel_id=1, source_target_pairs={{0,128},{64,192},{128,0},{192,64},{1,129},{65,193},{129,1},{193,65... | collective-permute-start | bytes 786440 | tf_op jit(solution)/shard_map/ppermute | solution.py:33
  9.9 38.2 %all-to-all-start = ((bf16[8,64,512]{2,1,0:T(8,128)(2,1)}), bf16[8,64,512]{2,1,0:T(8,128)(2,1)S(1)}, u32[]{:S(2)}, u32[]{:S(2)}) async-start(bf16[8,64,512]{2,1,0:T(8,128)(2,1)} %copies.1), calls=%async_computation | async-start | bytes 1048576 | tf_op jit(solution)/shard_map/all_to_all | solution.py:48
  18.5 20.2 %collective-permute-start.10 = (bf16[1032,256]{1,0:T(8,128)(2,1)S(1)}, bf16[1032,256]{1,0:T(8,128)(2,1)S(1)}, u32[]{:S(2)}, u32[]{:S(2)}) collective-permute-start(bf16[1032,256]{1,0:T(8,128)(2,1)S(1)} %pad_maximum_fusion.refs_5_.refs_6_), channel_id=1, source_target_pairs={{0,32},{16,51},{32,1},{48,16},{1,33},{17,48},{33,2},{49,17},{2,34}... | collective-permute-start | bytes 1585160 | tf_op jit(solution)/shard_map/ppermute | solution.py:44
  22.8 26.4 %collective-permute-start.22 = (bf16[384,1024]{1,0:T(8,128)(2,1)}, bf16[384,1024]{1,0:T(8,128)(2,1)}, u32[]{:S(2)}, u32[]{:S(2)}) collective-permute-start(bf16[384,1024]{1,0:T(8,128)(2,1)} %constant_dynamic-update-slice_fusion.refs_1_), channel_id=1, source_target_pairs={{0,4},{4,8},{8,12},{12,0},{1,5},{5,9},{9,13},{13,1},{2,6},{6,10},{... | collective-permute-start | bytes 2359304 | tf_op jit(solution)/shard_map/ppermute | solution.py:37
  24.1 25.7 %collective-permute-start.20 = (bf16[384,1024]{1,0:T(8,128)(2,1)}, bf16[384,1024]{1,0:T(8,128)(2,1)S(1)}, u32[]{:S(2)}, u32[]{:S(2)}) collective-permute-start(bf16[384,1024]{1,0:T(8,128)(2,1)} %constant_dynamic-update-slice_fusion.refs_1_), channel_id=1, source_target_pairs={{0,12},{4,0},{8,4},{12,8},{1,13},{5,1},{9,5},{13,9},{2,14},{6,2},{... | collective-permute-start | bytes 2359304 | tf_op jit(solution)/shard_map/ppermute | solution.py:37
  24.8 23.4 %collective-permute-start.21 = (bf16[128,1024]{1,0:T(8,128)(2,1)S(1)}, bf16[128,1024]{1,0:T(8,128)(2,1)}, u32[]{:S(2)}, u32[]{:S(2)}) collective-permute-start(bf16[128,1024]{1,0:T(8,128)(2,1)S(1)} %norm.1.refs_0_), channel_id=1, source_target_pairs={{0,4},{4,8},{8,12},{12,0},{1,5},{5,9},{9,13},{13,1},{2,6},{6,10},{... | collective-permute-start | bytes 786440 | tf_op jit(solution)/shard_map/ppermute | solution.py:37
  26.1 23.1 %collective-permute-start.19 = (bf16[128,1024]{1,0:T(8,128)(2,1)S(1)}, bf16[128,1024]{1,0:T(8,128)(2,1)}, u32[]{:S(2)}, u32[]{:S(2)}) collective-permute-start(bf16[128,1024]{1,0:T(8,128)(2,1)S(1)} %norm.1.refs_0_), channel_id=1, source_target_pairs={{0,12},{4,0},{8,4},{12,8},{1,13},{5,1},{9,5},{13,9},{2,14},{6,2},{... | collective-permute-start | bytes 786440 | tf_op jit(solution)/shard_map/ppermute | solution.py:37
  58.6 16.0 %collective-permute-start.4 = (bf16[8,64,512]{2,1,0:T(8,128)(2,1)S(1)}, bf16[8,64,512]{2,1,0:T(8,128)(2,1)S(1)}, u32[]{:S(2)}, u32[]{:S(2)}) collective-permute-start(bf16[8,64,512]{2,1,0:T(8,128)(2,1)S(1)} %collective-permute-done.3.refs_1_), channel_id=1, source_target_pairs={{0,64},{16,208},{64,128},{80,16},{128,192},{144,80},{192,0},{208,1... | collective-permute-start | bytes 1572872 | tf_op jit(solution)/shard_map/ppermute | solution.py:52
  59.1 15.6 %collective-permute-start.18 = (bf16[8,64,512]{2,1,0:T(8,128)(2,1)S(1)}, bf16[8,64,512]{2,1,0:T(8,128)(2,1)S(1)}, u32[]{:S(2)}, u32[]{:S(2)}) collective-permute-start(bf16[8,64,512]{2,1,0:T(8,128)(2,1)S(1)} %collective-permute-done.6.refs_2_), channel_id=1, source_target_pairs={{0,16},{16,0},{1,17},{17,1},{2,18},{18,2},{3,19},{19,3},{4,20},{20... | collective-permute-start | bytes 1572872 | tf_op jit(solution)/shard_map/ppermute | solution.py:56
  60.1 16.6 %collective-permute-start.13 = (bf16[1032,256]{1,0:T(8,128)(2,1)S(1)}, bf16[1032,256]{1,0:T(8,128)(2,1)S(1)}, u32[]{:S(2)}, u32[]{:S(2)}) collective-permute-start(bf16[1032,256]{1,0:T(8,128)(2,1)S(1)} %collective-permute-done.12.refs_11_.refs_9_), channel_id=1, source_target_pairs={{0,16},{16,0},{1,17},{17,1},{2,18},{18,2},{3,19},{19,3},{4,20},{20... | collective-permute-start | bytes 1585160 | tf_op jit(solution)/shard_map/ppermute | solution.py:56
  60.2 15.8 %collective-permute-start.14 = (bf16[520,256]{1,0:T(8,128)(2,1)S(1)}, bf16[520,256]{1,0:T(8,128)(2,1)S(1)}, u32[]{:S(2)}, u32[]{:S(2)}) collective-permute-start(bf16[520,256]{1,0:T(8,128)(2,1)S(1)} %slice.20), channel_id=1, source_target_pairs={{0,32},{16,51},{32,1},{48,16},{1,33},{17,48},{33,2},{49,17},{2,34}... | collective-permute-start | bytes 798728 | tf_op jit(solution)/shard_map/ppermute | solution.py:44
  74.6 14.4 %collective-permute-start.23 = (bf16[256,1024]{1,0:T(8,128)(2,1)S(1)}, bf16[256,1024]{1,0:T(8,128)(2,1)S(1)}, u32[]{:S(2)}, u32[]{:S(2)}) collective-permute-start(bf16[256,1024]{1,0:T(8,128)(2,1)S(1)} %pad_maximum_fusion.1), channel_id=1, source_target_pairs={{0,4},{4,8},{8,12},{12,0},{1,5},{5,9},{9,13},{13,1},{2,6},{6,10},{... | collective-permute-start | bytes 1572872 | tf_op jit(solution)/shard_map/ppermute | solution.py:37
  76.0 14.1 %collective-permute-start.24 = (bf16[256,1024]{1,0:T(8,128)(2,1)S(1)}, bf16[256,1024]{1,0:T(8,128)(2,1)S(1)}, u32[]{:S(2)}, u32[]{:S(2)}) collective-permute-start(bf16[256,1024]{1,0:T(8,128)(2,1)S(1)} %pad_maximum_fusion.2), channel_id=1, source_target_pairs={{0,12},{4,0},{8,4},{12,8},{1,13},{5,1},{9,5},{13,9},{2,14},{6,2},{... | collective-permute-start | bytes 1572872 | tf_op jit(solution)/shard_map/ppermute | solution.py:37
  95.3 19.0 %collective-permute-start.29 = (bf16[2,512,256]{2,1,0:T(8,128)(2,1)S(1)}, bf16[2,512,256]{2,1,0:T(8,128)(2,1)S(1)}, u32[]{:S(2)}, u32[]{:S(2)}) collective-permute-start(bf16[2,512,256]{2,1,0:T(8,128)(2,1)S(1)} %get-tuple-element.38), channel_id=1, source_target_pairs={{0,12},{4,0},{8,4},{12,8},{1,13},{5,1},{9,5},{13,9},{2,14},{6,2},{... | collective-permute-start | bytes 1572872 | tf_op jit(solution)/shard_map/ppermute | solution.py:37
  96.1 18.3 %collective-permute-start.25 = (bf16[2,512,256]{2,1,0:T(8,128)(2,1)S(1)}, bf16[2,512,256]{2,1,0:T(8,128)(2,1)S(1)}, u32[]{:S(2)}, u32[]{:S(2)}) collective-permute-start(bf16[2,512,256]{2,1,0:T(8,128)(2,1)S(1)} %get-tuple-element.34), channel_id=1, source_target_pairs={{0,4},{4,8},{8,12},{12,0},{1,5},{5,9},{9,13},{13,1},{2,6},{6,10},{... | collective-permute-start | bytes 1572872 | tf_op jit(solution)/shard_map/ppermute | solution.py:37
  104.6 17.5 %collective-permute-start.27 = (bf16[2,512,256]{2,1,0:T(8,128)(2,1)S(1)}, bf16[2,512,256]{2,1,0:T(8,128)(2,1)S(1)}, u32[]{:S(2)}, u32[]{:S(2)}) collective-permute-start(bf16[2,512,256]{2,1,0:T(8,128)(2,1)S(1)} %get-tuple-element.35), channel_id=1, source_target_pairs={{0,12},{4,0},{8,4},{12,8},{1,13},{5,1},{9,5},{13,9},{2,14},{6,2},{... | collective-permute-start | bytes 1572872 | tf_op jit(solution)/shard_map/ppermute | solution.py:37
  111.0 22.9 %collective-permute-start.28 = (bf16[2,512,256]{2,1,0:T(8,128)(2,1)S(1)}, bf16[2,512,256]{2,1,0:T(8,128)(2,1)S(1)}, u32[]{:S(2)}, u32[]{:S(2)}) collective-permute-start(bf16[2,512,256]{2,1,0:T(8,128)(2,1)S(1)} %get-tuple-element.36), channel_id=1, source_target_pairs={{0,4},{4,8},{8,12},{12,0},{1,5},{5,9},{9,13},{13,1},{2,6},{6,10},{... | collective-permute-start | bytes 1572872 | tf_op jit(solution)/shard_map/ppermute | solution.py:37
  114.3 19.6 %collective-permute-start.35 = (bf16[512,256]{1,0:T(8,128)(2,1)S(1)}, bf16[512,256]{1,0:T(8,128)(2,1)S(1)}, u32[]{:S(2)}, u32[]{:S(2)}) collective-permute-start(bf16[512,256]{1,0:T(8,128)(2,1)S(1)} %add_in.7), channel_id=1, source_target_pairs={{0,12},{4,0},{8,4},{12,8},{1,13},{5,1},{9,5},{13,9},{2,14},{6,2},{... | collective-permute-start | bytes 786440 | tf_op jit(solution)/shard_map/ppermute | solution.py:37
  114.5 19.4 %collective-permute-start.34 = (bf16[512,256]{1,0:T(8,128)(2,1)S(1)}, bf16[512,256]{1,0:T(8,128)(2,1)S(1)}, u32[]{:S(2)}, u32[]{:S(2)}) collective-permute-start(bf16[512,256]{1,0:T(8,128)(2,1)S(1)} %add_in.6), channel_id=1, source_target_pairs={{0,4},{4,8},{8,12},{12,0},{1,5},{5,9},{9,13},{13,1},{2,6},{6,10},{... | collective-permute-start | bytes 786440 | tf_op jit(solution)/shard_map/ppermute | solution.py:37
  117.9 19.6 %collective-permute-start.30 = (bf16[512,256]{1,0:T(8,128)(2,1)S(1)}, bf16[512,256]{1,0:T(8,128)(2,1)S(1)}, u32[]{:S(2)}, u32[]{:S(2)}) collective-permute-start(bf16[512,256]{1,0:T(8,128)(2,1)S(1)} %add_in.5), channel_id=1, source_target_pairs={{0,12},{4,0},{8,4},{12,8},{1,13},{5,1},{9,5},{13,9},{2,14},{6,2},{... | collective-permute-start | bytes 786440 | tf_op jit(solution)/shard_map/ppermute | solution.py:37
  122.1 15.5 %collective-permute-start.26 = (bf16[512,256]{1,0:T(8,128)(2,1)S(1)}, bf16[512,256]{1,0:T(8,128)(2,1)S(1)}, u32[]{:S(2)}, u32[]{:S(2)}) collective-permute-start(bf16[512,256]{1,0:T(8,128)(2,1)S(1)} %add_in.4), channel_id=1, source_target_pairs={{0,4},{4,8},{8,12},{12,0},{1,5},{5,9},{9,13},{13,1},{2,6},{6,10},{... | collective-permute-start | bytes 786440 | tf_op jit(solution)/shard_map/ppermute | solution.py:37
  (23 other events, 189.1 us)

commit v2 on v1

--- a/solution.py
+++ b/solution.py
@@ -25,8 +25,8 @@
     return [(i, (i + d) % n) for i in range(n)]
 
 
-def both_ways(n):
-    return [(2 * i + c, 2 * ((i + (1 - 2 * c)) % n) + c) for i in range(n) for c in (0, 1)]
+def both_ways(n, d=1):
+    return [(2 * i + c, 2 * ((i + d - 2 * d * c) % n) + c) for i in range(n) for c in (0, 1)]
 
 
 def on_x(a, d):
@@ -37,11 +37,11 @@
     return lax.ppermute(a, "y", ring(Y, d))
 
 
-def on_z(a):
+def on_z(a, d):
     def at(i):
         return (i // 2 % 2 * 2 + i % 2) * ZH + i // 4
 
-    return lax.ppermute(a, ("zl", "c", "zh"), [(at(i), at(j)) for i, j in both_ways(Z)])
+    return lax.ppermute(a, ("zl", "c", "zh"), [(at(i), at(j)) for i, j in both_ways(Z, d)])
 
 
 def over_z(a):
@@ -251,7 +251,7 @@
         in_specs=[VMEM] * (len(toks) + 3),
         out_specs=(VMEM, VMEM),
         scratch_shapes=[pltpu.VMEM((512, D), BF), pltpu.VMEM((256, HID), BF)],
-        compiler_params=pltpu.CompilerParams(vmem_limit_bytes=20 * 2**20),
+        compiler_params=pltpu.CompilerParams(vmem_limit_bytes=12 * 2**20),
         name="mlp",
         cost_estimate=pl.CostEstimate(
             flops=10**8, bytes_accessed=2**23, transcendentals=512 * HID
@@ -353,9 +353,8 @@
 
     d_other = on_c(down_weight)
     w = [jnp.concatenate([down_weight, split_bias(up_bias), d_other], axis=0)]
-    for _ in range(3):
-        w.append(on_z(w[-1]))
-    w.append(on_z(w[3][: GROUP + 8]))
+    w += [on_z(w[0], 1), on_z(w[0], 2)]
+    w += [on_z(w[2], 1), on_z(w[2][: GROUP + 8], 2)]
     pieces |= dict(w0=w[0], e0=d_other)
     for k, a in enumerate(w[1:], 1):
         pieces |= {f"w{k}": a, f"e{k}": on_c(a)}

time: 153 us -> 165 us (1.078)
  the two profiles are of different devices: /device:TPU:16 before, /device:TPU:32 now
where the time goes in v2:
time: 165 us; the launch traced here: 164 us
  waiting for transfers between devices  66.4 us (40%)
  starting transfers between devices  60 us (36%)
  Pallas kernels  29.9 us (18%)
  local copies, waits for them, and re-layouts  7.33 us (4%)
    ppermute x14, waiting for transfers between devices, on_y(): return lax.ppermute(a, 'y', ring(Y, d))  38.8 us
    pallas_call x4, Pallas kernels, mlp(): pl.pallas_call(functools.partial(kernel, plan), out_shape=(half, half), i...  25.6 us
    ppermute x14, starting transfers between devices, on_y(): return lax.ppermute(a, 'y', ring(Y, d))  23.8 us
    ppermute x9, starting transfers between devices, on_x(): return lax.ppermute(a, 'x', ring(X, d))  13.5 us
    ppermute x4, waiting for transfers between devices, on_z(): lax.ppermute(a, ('zl', 'c', 'zh'), [(at(i), at(j)) for i, j in both_ways(...  11.8 us
    ppermute x3, waiting for transfers between devices, on_xc(): return lax.ppermute(a, ('x', 'c'), both_ways(X))  10.4 us
    ppermute x4, starting transfers between devices, on_z(): lax.ppermute(a, ('zl', 'c', 'zh'), [(at(i), at(j)) for i, j in both_ways(...  9.81 us
    all_to_all x1, starting transfers between devices, over_z(): lax.all_to_all(a, ('zl', 'zh'), split_axis=0, concat_axis=0, tiled=True)  8.7 us
  transfers between devices with their start and end apart: 40, of which 14 were waited for; matrix products, arithmetic and copies ran while one was open for 3% of the time, Pallas kernels for 14%

profile of v2, /device:TPU:32, one launch (start us, length us, event | category | flops | bytes accessed | tf_op | source)
XLA Modules:
  0.0 164.2 jit_solution(4679194707024943870)
XLA Ops:
  4.7 1.7 %collective-permute-start.1 = (bf16[128,1024]{1,0:T(8,128)(2,1)S(1)}, bf16[128,1024]{1,0:T(8,128)(2,1)S(1)}, u32[]{:S(2)}, u32[]{:S(2)}) collective-permute-start(bf16[128,1024]{1,0:T(8,128)(2,1)S(1)} %norm.1.refs_0_), channel_id=1, source_target_pairs={{0,192},{64,0},{128,64},{192,128},{1,193},{65,1},{129,65},{193,129... | collective-permute-start | bytes 786440 | tf_op jit(solution)/shard_map/ppermute | solution.py:33
  6.4 1.8 %collective-permute-start.2 = (bf16[128,1024]{1,0:T(8,128)(2,1)S(1)}, bf16[128,1024]{1,0:T(8,128)(2,1)S(1)}, u32[]{:S(2)}, u32[]{:S(2)}) collective-permute-start(bf16[128,1024]{1,0:T(8,128)(2,1)S(1)} %norm.1.refs_0_), channel_id=1, source_target_pairs={{0,128},{64,192},{128,0},{192,64},{1,129},{65,193},{129,1},{193,65... | collective-permute-start | bytes 786440 | tf_op jit(solution)/shard_map/ppermute | solution.py:33
  9.9 8.7 %all-to-all-start = ((bf16[8,64,512]{2,1,0:T(8,128)(2,1)}), bf16[8,64,512]{2,1,0:T(8,128)(2,1)S(1)}, u32[]{:S(2)}, u32[]{:S(2)}) async-start(bf16[8,64,512]{2,1,0:T(8,128)(2,1)} %copies.1), calls=%async_computation | async-start | bytes 1048576 | tf_op jit(solution)/shard_map/all_to_all | solution.py:48
  22.5 2.4 %collective-permute-start.10 = (bf16[1032,256]{1,0:T(8,128)(2,1)S(1)}, bf16[1032,256]{1,0:T(8,128)(2,1)S(1)}, u32[]{:S(2)}, u32[]{:S(2)}) collective-permute-start(bf16[1032,256]{1,0:T(8,128)(2,1)S(1)} %pad_maximum_fusion.refs_5_.refs_6_), channel_id=1, source_target_pairs={{0,1},{16,19},{32,33},{48,51},{1,2},{17,16},{33,34},{49,48},{2,3},... | collective-permute-start | bytes 1585160 | tf_op jit(solution)/shard_map/ppermute | solution.py:44
  28.1 3.0 %collective-permute-start.15 = (bf16[1032,256]{1,0:T(8,128)(2,1)S(1)}, bf16[1032,256]{1,0:T(8,128)(2,1)S(1)}, u32[]{:S(2)}, u32[]{:S(2)}) collective-permute-start(bf16[1032,256]{1,0:T(8,128)(2,1)S(1)} %pad_maximum_fusion.refs_5_.refs_6_), channel_id=1, source_target_pairs={{0,32},{16,51},{32,1},{48,16},{1,33},{17,48},{33,2},{49,17},{2,34}... | collective-permute-start | bytes 1585160 | tf_op jit(solution)/shard_map/ppermute | solution.py:44
  31.1 16.2 %collective-permute-done.21.refs_0_ = bf16[128,1024]{1,0:T(8,128)(2,1)S(1)} collective-permute-done((bf16[128,1024]{1,0:T(8,128)(2,1)S(1)}, bf16[128,1024]{1,0:T(8,128)(2,1)S(1)}, u32[]{:S(2)}, u32[]{:S(2)}) %collective-permute-start.21) | collective-permute-done | bytes 262176 | tf_op jit(solution)/shard_map/ppermute | solution.py:37
  49.1 5.7 %collective-permute-done.19.refs_0_ = bf16[128,1024]{1,0:T(8,128)(2,1)} collective-permute-done((bf16[128,1024]{1,0:T(8,128)(2,1)S(1)}, bf16[128,1024]{1,0:T(8,128)(2,1)}, u32[]{:S(2)}, u32[]{:S(2)}) %collective-permute-start.19) | collective-permute-done | bytes 262176 | tf_op jit(solution)/shard_map/ppermute | solution.py:37
  57.0 2.9 %collective-permute-start.13 = (bf16[520,256]{1,0:T(8,128)(2,1)S(1)}, bf16[520,256]{1,0:T(8,128)(2,1)S(1)}, u32[]{:S(2)}, u32[]{:S(2)}) collective-permute-start(bf16[520,256]{1,0:T(8,128)(2,1)S(1)} %slice.20), channel_id=1, source_target_pairs={{0,1},{16,19},{32,33},{48,51},{1,2},{17,16},{33,34},{49,48},{2,3},... | collective-permute-start | bytes 798728 | tf_op jit(solution)/shard_map/ppermute | solution.py:44
  59.9 11.8 %collective-permute-done.13.refs_4_.refs_10_ = bf16[520,256]{1,0:T(8,128)(2,1)S(1)} collective-permute-done((bf16[520,256]{1,0:T(8,128)(2,1)S(1)}, bf16[520,256]{1,0:T(8,128)(2,1)S(1)}, u32[]{:S(2)}, u32[]{:S(2)}) %collective-permute-start.13) | collective-permute-done | bytes 266272 | tf_op jit(solution)/shard_map/ppermute | solution.py:44
  77.3 4.8 %collective-permute-done.7.refs_1_ = bf16[8,64,512]{2,1,0:T(8,128)(2,1)S(1)} collective-permute-done((bf16[8,64,512]{2,1,0:T(8,128)(2,1)S(1)}, bf16[8,64,512]{2,1,0:T(8,128)(2,1)S(1)}, u32[]{:S(2)}, u32[]{:S(2)}) %collective-permute-start.7) | collective-permute-done | bytes 524320 | tf_op jit(solution)/shard_map/ppermute | solution.py:52
  82.0 5.6 %collective-permute-done.4.refs_3_ = bf16[8,64,512]{2,1,0:T(8,128)(2,1)S(1)} collective-permute-done((bf16[8,64,512]{2,1,0:T(8,128)(2,1)S(1)}, bf16[8,64,512]{2,1,0:T(8,128)(2,1)S(1)}, u32[]{:S(2)}, u32[]{:S(2)}) %collective-permute-start.4) | collective-permute-done | bytes 524320 | tf_op jit(solution)/shard_map/ppermute | solution.py:52
  88.1 2.9 %collective-permute-start.24 = (bf16[256,1024]{1,0:T(8,128)(2,1)S(1)}, bf16[256,1024]{1,0:T(8,128)(2,1)S(1)}, u32[]{:S(2)}, u32[]{:S(2)}) collective-permute-start(bf16[256,1024]{1,0:T(8,128)(2,1)S(1)} %pad_maximum_fusion.2), channel_id=1, source_target_pairs={{0,12},{4,0},{8,4},{12,8},{1,13},{5,1},{9,5},{13,9},{2,14},{6,2},{... | collective-permute-start | bytes 1572872 | tf_op jit(solution)/shard_map/ppermute | solution.py:37
  91.9 11.4 %collective-permute-done.23.refs_0_ = bf16[256,1024]{1,0:T(8,128)(2,1)S(1)} collective-permute-done((bf16[256,1024]{1,0:T(8,128)(2,1)S(1)}, bf16[256,1024]{1,0:T(8,128)(2,1)S(1)}, u32[]{:S(2)}, u32[]{:S(2)}) %collective-permute-start.23) | collective-permute-done | bytes 524320 | tf_op jit(solution)/shard_map/ppermute | solution.py:37
  103.4 5.3 %mlp.6 = (bf16[2,512,256]{2,1,0:T(8,128)(2,1)S(1)}, bf16[2,512,256]{2,1,0:T(8,128)(2,1)S(1)}) custom-call(bf16[256,1024]{1,0:T(8,128)(2,1)S(1)} %collective-permute-done.23.refs_0_, bf16[256,1024]{1,0:T(8,128)(2,1)S(1)} %collective-permute-done.24.refs_1_, bf16[4,1024,512]{2,1,0:T(8,128)(2,1)S(1)} %get-tuple-element.28.refs_2_, ...), custom_call_target="tpu_custom_call" | custom-call | flops 100000000 | bytes 8388608 | tf_op jit(solution)/shard_map/mlp/pallas_call | solution.py:248
  108.7 3.1 %collective-permute-start.29 = (bf16[2,512,256]{2,1,0:T(8,128)(2,1)S(1)}, bf16[2,512,256]{2,1,0:T(8,128)(2,1)S(1)}, u32[]{:S(2)}, u32[]{:S(2)}) collective-permute-start(bf16[2,512,256]{2,1,0:T(8,128)(2,1)S(1)} %get-tuple-element.38), channel_id=1, source_target_pairs={{0,12},{4,0},{8,4},{12,8},{1,13},{5,1},{9,5},{13,9},{2,14},{6,2},{... | collective-permute-start | bytes 1572872 | tf_op jit(solution)/shard_map/ppermute | solution.py:37
  111.8 5.3 %mlp.7 = (bf16[2,512,256]{2,1,0:T(8,128)(2,1)S(1)}, bf16[2,512,256]{2,1,0:T(8,128)(2,1)S(1)}) custom-call(bf16[128,1024]{1,0:T(8,128)(2,1)S(1)} %copy-done.1, bf16[384,1024]{1,0:T(8,128)(2,1)S(1)} %collective-permute-done.22.refs_1_, bf16[4,1024,512]{2,1,0:T(8,128)(2,1)S(1)} %get-tuple-element.28.refs_2_, f32[4,512]{1,0:T(4,128)S(1)} %get-tuple-element.29.refs_3_, ...), custom_call_target="tpu_custom_call" | custom-call | flops 100000000 | bytes 8388608 | tf_op jit(solution)/shard_map/mlp/pallas_call | solution.py:248
  117.1 3.5 %collective-permute-start.27 = (bf16[2,512,256]{2,1,0:T(8,128)(2,1)S(1)}, bf16[2,512,256]{2,1,0:T(8,128)(2,1)S(1)}, u32[]{:S(2)}, u32[]{:S(2)}) collective-permute-start(bf16[2,512,256]{2,1,0:T(8,128)(2,1)S(1)} %get-tuple-element.35), channel_id=1, source_target_pairs={{0,12},{4,0},{8,4},{12,8},{1,13},{5,1},{9,5},{13,9},{2,14},{6,2},{... | collective-permute-start | bytes 1572872 | tf_op jit(solution)/shard_map/ppermute | solution.py:37
  120.6 6.5 %mlp.5 = (bf16[2,512,256]{2,1,0:T(8,128)(2,1)S(1)}, bf16[2,512,256]{2,1,0:T(8,128)(2,1)S(1)}) custom-call(bf16[128,1024]{1,0:T(8,128)(2,1)} %collective-permute-done.19.refs_0_, bf16[384,1024]{1,0:T(8,128)(2,1)} %collective-permute-done.20.refs_1_, bf16[4,1024,512]{2,1,0:T(8,128)(2,1)S(1)} %get-tuple-element.28.refs_2_, ...), custom_call_target="tpu_custom_call" | custom-call | flops 100000000 | bytes 8388608 | tf_op jit(solution)/shard_map/mlp/pallas_call | solution.py:248
  127.3 3.3 %collective-permute-start.35 = (bf16[512,256]{1,0:T(8,128)(2,1)S(1)}, bf16[512,256]{1,0:T(8,128)(2,1)S(1)}, u32[]{:S(2)}, u32[]{:S(2)}) collective-permute-start(bf16[512,256]{1,0:T(8,128)(2,1)S(1)} %add_in.7), channel_id=1, source_target_pairs={{0,12},{4,0},{8,4},{12,8},{1,13},{5,1},{9,5},{13,9},{2,14},{6,2},{... | collective-permute-start | bytes 786440 | tf_op jit(solution)/shard_map/ppermute | solution.py:37
  130.9 3.3 %collective-permute-start.30 = (bf16[512,256]{1,0:T(8,128)(2,1)S(1)}, bf16[512,256]{1,0:T(8,128)(2,1)S(1)}, u32[]{:S(2)}, u32[]{:S(2)}) collective-permute-start(bf16[512,256]{1,0:T(8,128)(2,1)S(1)} %add_in.5), channel_id=1, source_target_pairs={{0,12},{4,0},{8,4},{12,8},{1,13},{5,1},{9,5},{13,9},{2,14},{6,2},{... | collective-permute-start | bytes 786440 | tf_op jit(solution)/shard_map/ppermute | solution.py:37
  135.9 8.6 %mlp.4 = (bf16[2,512,256]{2,1,0:T(8,128)(2,1)S(1)}, bf16[2,512,256]{2,1,0:T(8,128)(2,1)S(1)}) custom-call(bf16[128,1024]{1,0:T(8,128)(2,1)S(1)} %norm.1.refs_0_, bf16[384,1024]{1,0:T(8,128)(2,1)} %constant_dynamic-update-slice_fusion.refs_1_, bf16[4,1024,512]{2,1,0:T(8,128)(2,1)S(1)} %get-tuple-element.28.refs_2_, f32[4,512]{1,0:T(4,128)S(1)} %get-tuple-element.29.refs_3_, ...), custom_call_target="tpu_custom_call" | custom-call | flops 100000000 | bytes 8388608 | tf_op jit(solution)/shard_map/mlp/pallas_call | solution.py:248
  144.5 4.3 %collective-permute-done.34.sum0 = bf16[512,256]{1,0:T(8,128)(2,1)S(1)} collective-permute-done((bf16[512,256]{1,0:T(8,128)(2,1)S(1)}, bf16[512,256]{1,0:T(8,128)(2,1)S(1)}, u32[]{:S(2)}, u32[]{:S(2)}) %collective-permute-start.34) | collective-permute-done | bytes 262176 | tf_op jit(solution)/shard_map/ppermute | solution.py:37
  149.2 3.2 %collective-permute-start.37 = (bf16[2,128,256]{2,1,0:T(8,128)(2,1)S(1)}, bf16[2,128,256]{2,1,0:T(8,128)(2,1)S(1)}, u32[]{:S(2)}, u32[]{:S(2)}) collective-permute-start(bf16[2,128,256]{2,1,0:T(8,128)(2,1)S(1)} %get-tuple-element.45), channel_id=1, source_target_pairs={{0,192},{64,0},{128,64},{192,128},{1,193},{65,1},{129,65},{193,129... | collective-permute-start | bytes 393224 | tf_op jit(solution)/shard_map/ppermute | solution.py:33
  153.9 2.1 %collective-permute-start.32 = (bf16[2,128,256]{2,1,0:T(8,128)(2,1)S(1)}, bf16[2,128,256]{2,1,0:T(8,128)(2,1)S(1)}, u32[]{:S(2)}, u32[]{:S(2)}) collective-permute-start(bf16[2,128,256]{2,1,0:T(8,128)(2,1)S(1)} %get-tuple-element.41), channel_id=1, source_target_pairs={{0,192},{64,0},{128,64},{192,128},{1,193},{65,1},{129,65},{193,129... | collective-permute-start | bytes 393224 | tf_op jit(solution)/shard_map/ppermute | solution.py:33
  (102 shorter events, 36.2 us)
Async XLA Ops:
  3.1 15.5 %collective-permute-start = (bf16[128,1024]{1,0:T(8,128)(2,1)S(1)}, bf16[128,1024]{1,0:T(8,128)(2,1)S(1)}, u32[]{:S(2)}, u32[]{:S(2)}) collective-permute-start(bf16[128,1024]{1,0:T(8,128)(2,1)S(1)} %norm.1.refs_0_), channel_id=1, source_target_pairs={{0,64},{64,128},{128,192},{192,0},{1,65},{65,129},{129,193},{193,1... | collective-permute-start | bytes 786440 | tf_op jit(solution)/shard_map/ppermute | solution.py:33
  9.9 44.9 %all-to-all-start = ((bf16[8,64,512]{2,1,0:T(8,128)(2,1)}), bf16[8,64,512]{2,1,0:T(8,128)(2,1)S(1)}, u32[]{:S(2)}, u32[]{:S(2)}) async-start(bf16[8,64,512]{2,1,0:T(8,128)(2,1)} %copies.1), calls=%async_computation | async-start | bytes 1048576 | tf_op jit(solution)/shard_map/all_to_all | solution.py:48
  20.8 36.1 %collective-permute-start.22 = (bf16[384,1024]{1,0:T(8,128)(2,1)}, bf16[384,1024]{1,0:T(8,128)(2,1)S(1)}, u32[]{:S(2)}, u32[]{:S(2)}) collective-permute-start(bf16[384,1024]{1,0:T(8,128)(2,1)} %constant_dynamic-update-slice_fusion.refs_1_), channel_id=1, source_target_pairs={{0,4},{4,8},{8,12},{12,0},{1,5},{5,9},{9,13},{13,1},{2,6},{6,10},{... | collective-permute-start | bytes 2359304 | tf_op jit(solution)/shard_map/ppermute | solution.py:37
  22.5 32.9 %collective-permute-start.10 = (bf16[1032,256]{1,0:T(8,128)(2,1)S(1)}, bf16[1032,256]{1,0:T(8,128)(2,1)S(1)}, u32[]{:S(2)}, u32[]{:S(2)}) collective-permute-start(bf16[1032,256]{1,0:T(8,128)(2,1)S(1)} %pad_maximum_fusion.refs_5_.refs_6_), channel_id=1, source_target_pairs={{0,1},{16,19},{32,33},{48,51},{1,2},{17,16},{33,34},{49,48},{2,3},... | collective-permute-start | bytes 1585160 | tf_op jit(solution)/shard_map/ppermute | solution.py:44
  24.9 22.4 %collective-permute-start.21 = (bf16[128,1024]{1,0:T(8,128)(2,1)S(1)}, bf16[128,1024]{1,0:T(8,128)(2,1)S(1)}, u32[]{:S(2)}, u32[]{:S(2)}) collective-permute-start(bf16[128,1024]{1,0:T(8,128)(2,1)S(1)} %norm.1.refs_0_), channel_id=1, source_target_pairs={{0,4},{4,8},{8,12},{12,0},{1,5},{5,9},{9,13},{13,1},{2,6},{6,10},{... | collective-permute-start | bytes 786440 | tf_op jit(solution)/shard_map/ppermute | solution.py:37
  26.5 33.4 %collective-permute-start.20 = (bf16[384,1024]{1,0:T(8,128)(2,1)}, bf16[384,1024]{1,0:T(8,128)(2,1)}, u32[]{:S(2)}, u32[]{:S(2)}) collective-permute-start(bf16[384,1024]{1,0:T(8,128)(2,1)} %constant_dynamic-update-slice_fusion.refs_1_), channel_id=1, source_target_pairs={{0,12},{4,0},{8,4},{12,8},{1,13},{5,1},{9,5},{13,9},{2,14},{6,2},{... | collective-permute-start | bytes 2359304 | tf_op jit(solution)/shard_map/ppermute | solution.py:37
  28.1 27.3 %collective-permute-start.15 = (bf16[1032,256]{1,0:T(8,128)(2,1)S(1)}, bf16[1032,256]{1,0:T(8,128)(2,1)S(1)}, u32[]{:S(2)}, u32[]{:S(2)}) collective-permute-start(bf16[1032,256]{1,0:T(8,128)(2,1)S(1)} %pad_maximum_fusion.refs_5_.refs_6_), channel_id=1, source_target_pairs={{0,32},{16,51},{32,1},{48,16},{1,33},{17,48},{33,2},{49,17},{2,34}... | collective-permute-start | bytes 1585160 | tf_op jit(solution)/shard_map/ppermute | solution.py:44
  54.8 16.8 %collective-permute-start.6 = (bf16[8,64,512]{2,1,0:T(8,128)(2,1)S(1)}, bf16[8,64,512]{2,1,0:T(8,128)(2,1)S(1)}, u32[]{:S(2)}, u32[]{:S(2)}) collective-permute-start(bf16[8,64,512]{2,1,0:T(8,128)(2,1)S(1)} %all-to-all-done.refs_0_), channel_id=1, source_target_pairs={{0,64},{16,208},{64,128},{80,16},{128,192},{144,80},{192,0},{208,1... | collective-permute-start | bytes 1572872 | tf_op jit(solution)/shard_map/ppermute | solution.py:52
  55.4 17.3 %collective-permute-start.3 = (bf16[8,64,512]{2,1,0:T(8,128)(2,1)S(1)}, bf16[8,64,512]{2,1,0:T(8,128)(2,1)S(1)}, u32[]{:S(2)}, u32[]{:S(2)}) collective-permute-start(bf16[8,64,512]{2,1,0:T(8,128)(2,1)S(1)} %all-to-all-done.refs_0_), channel_id=1, source_target_pairs={{0,16},{16,0},{1,17},{17,1},{2,18},{18,2},{3,19},{19,3},{4,20},{20... | collective-permute-start | bytes 1572872 | tf_op jit(solution)/shard_map/ppermute | solution.py:56
  55.4 17.7 %collective-permute-start.11 = (bf16[1032,256]{1,0:T(8,128)(2,1)S(1)}, bf16[1032,256]{1,0:T(8,128)(2,1)S(1)}, u32[]{:S(2)}, u32[]{:S(2)}) collective-permute-start(bf16[1032,256]{1,0:T(8,128)(2,1)S(1)} %collective-permute-done.10.refs_8_), channel_id=1, source_target_pairs={{0,32},{16,51},{32,1},{48,16},{1,33},{17,48},{33,2},{49,17},{2,34}... | collective-permute-start | bytes 1585160 | tf_op jit(solution)/shard_map/ppermute | solution.py:44
  59.9 14.8 %collective-permute-start.17 = (bf16[1032,256]{1,0:T(8,128)(2,1)S(1)}, bf16[1032,256]{1,0:T(8,128)(2,1)S(1)}, u32[]{:S(2)}, u32[]{:S(2)}) collective-permute-start(bf16[1032,256]{1,0:T(8,128)(2,1)S(1)} %collective-permute-done.10.refs_8_), channel_id=1, source_target_pairs={{0,16},{16,0},{1,17},{17,1},{2,18},{18,2},{3,19},{19,3},{4,20},{20... | collective-permute-start | bytes 1585160 | tf_op jit(solution)/shard_map/ppermute | solution.py:56
  72.7 14.9 %collective-permute-start.4 = (bf16[8,64,512]{2,1,0:T(8,128)(2,1)S(1)}, bf16[8,64,512]{2,1,0:T(8,128)(2,1)S(1)}, u32[]{:S(2)}, u32[]{:S(2)}) collective-permute-start(bf16[8,64,512]{2,1,0:T(8,128)(2,1)S(1)} %collective-permute-done.3.refs_1_), channel_id=1, source_target_pairs={{0,64},{16,208},{64,128},{80,16},{128,192},{144,80},{192,0},{208,1... | collective-permute-start | bytes 1572872 | tf_op jit(solution)/shard_map/ppermute | solution.py:52
  73.1 15.1 %collective-permute-start.18 = (bf16[8,64,512]{2,1,0:T(8,128)(2,1)S(1)}, bf16[8,64,512]{2,1,0:T(8,128)(2,1)S(1)}, u32[]{:S(2)}, u32[]{:S(2)}) collective-permute-start(bf16[8,64,512]{2,1,0:T(8,128)(2,1)S(1)} %collective-permute-done.6.refs_2_), channel_id=1, source_target_pairs={{0,16},{16,0},{1,17},{17,1},{2,18},{18,2},{3,19},{19,3},{4,20},{20... | collective-permute-start | bytes 1572872 | tf_op jit(solution)/shard_map/ppermute | solution.py:56
  76.8 14.8 %collective-permute-start.12 = (bf16[1032,256]{1,0:T(8,128)(2,1)S(1)}, bf16[1032,256]{1,0:T(8,128)(2,1)S(1)}, u32[]{:S(2)}, u32[]{:S(2)}) collective-permute-start(bf16[1032,256]{1,0:T(8,128)(2,1)S(1)} %collective-permute-done.11.refs_11_.refs_9_), channel_id=1, source_target_pairs={{0,16},{16,0},{1,17},{17,1},{2,18},{18,2},{3,19},{19,3},{4,20},{20... | collective-permute-start | bytes 1585160 | tf_op jit(solution)/shard_map/ppermute | solution.py:56
  87.7 15.7 %collective-permute-start.23 = (bf16[256,1024]{1,0:T(8,128)(2,1)S(1)}, bf16[256,1024]{1,0:T(8,128)(2,1)S(1)}, u32[]{:S(2)}, u32[]{:S(2)}) collective-permute-start(bf16[256,1024]{1,0:T(8,128)(2,1)S(1)} %pad_maximum_fusion.1), channel_id=1, source_target_pairs={{0,4},{4,8},{8,12},{12,0},{1,5},{5,9},{9,13},{13,1},{2,6},{6,10},{... | collective-permute-start | bytes 1572872 | tf_op jit(solution)/shard_map/ppermute | solution.py:37
  88.1 15.2 %collective-permute-start.24 = (bf16[256,1024]{1,0:T(8,128)(2,1)S(1)}, bf16[256,1024]{1,0:T(8,128)(2,1)S(1)}, u32[]{:S(2)}, u32[]{:S(2)}) collective-permute-start(bf16[256,1024]{1,0:T(8,128)(2,1)S(1)} %pad_maximum_fusion.2), channel_id=1, source_target_pairs={{0,12},{4,0},{8,4},{12,8},{1,13},{5,1},{9,5},{13,9},{2,14},{6,2},{... | collective-permute-start | bytes 1572872 | tf_op jit(solution)/shard_map/ppermute | solution.py:37
  108.7 18.6 %collective-permute-start.29 = (bf16[2,512,256]{2,1,0:T(8,128)(2,1)S(1)}, bf16[2,512,256]{2,1,0:T(8,128)(2,1)S(1)}, u32[]{:S(2)}, u32[]{:S(2)}) collective-permute-start(bf16[2,512,256]{2,1,0:T(8,128)(2,1)S(1)} %get-tuple-element.38), channel_id=1, source_target_pairs={{0,12},{4,0},{8,4},{12,8},{1,13},{5,1},{9,5},{13,9},{2,14},{6,2},{... | collective-permute-start | bytes 1572872 | tf_op jit(solution)/shard_map/ppermute | solution.py:37
  111.8 18.8 %collective-permute-start.25 = (bf16[2,512,256]{2,1,0:T(8,128)(2,1)S(1)}, bf16[2,512,256]{2,1,0:T(8,128)(2,1)S(1)}, u32[]{:S(2)}, u32[]{:S(2)}) collective-permute-start(bf16[2,512,256]{2,1,0:T(8,128)(2,1)S(1)} %get-tuple-element.34), channel_id=1, source_target_pairs={{0,4},{4,8},{8,12},{12,0},{1,5},{5,9},{9,13},{13,1},{2,6},{6,10},{... | collective-permute-start | bytes 1572872 | tf_op jit(solution)/shard_map/ppermute | solution.py:37
  117.1 18.3 %collective-permute-start.27 = (bf16[2,512,256]{2,1,0:T(8,128)(2,1)S(1)}, bf16[2,512,256]{2,1,0:T(8,128)(2,1)S(1)}, u32[]{:S(2)}, u32[]{:S(2)}) collective-permute-start(bf16[2,512,256]{2,1,0:T(8,128)(2,1)S(1)} %get-tuple-element.35), channel_id=1, source_target_pairs={{0,12},{4,0},{8,4},{12,8},{1,13},{5,1},{9,5},{13,9},{2,14},{6,2},{... | collective-permute-start | bytes 1572872 | tf_op jit(solution)/shard_map/ppermute | solution.py:37
  127.1 17.4 %collective-permute-start.28 = (bf16[2,512,256]{2,1,0:T(8,128)(2,1)S(1)}, bf16[2,512,256]{2,1,0:T(8,128)(2,1)S(1)}, u32[]{:S(2)}, u32[]{:S(2)}) collective-permute-start(bf16[2,512,256]{2,1,0:T(8,128)(2,1)S(1)} %get-tuple-element.36), channel_id=1, source_target_pairs={{0,4},{4,8},{8,12},{12,0},{1,5},{5,9},{9,13},{13,1},{2,6},{6,10},{... | collective-permute-start | bytes 1572872 | tf_op jit(solution)/shard_map/ppermute | solution.py:37
  127.3 17.2 %collective-permute-start.35 = (bf16[512,256]{1,0:T(8,128)(2,1)S(1)}, bf16[512,256]{1,0:T(8,128)(2,1)S(1)}, u32[]{:S(2)}, u32[]{:S(2)}) collective-permute-start(bf16[512,256]{1,0:T(8,128)(2,1)S(1)} %add_in.7), channel_id=1, source_target_pairs={{0,12},{4,0},{8,4},{12,8},{1,13},{5,1},{9,5},{13,9},{2,14},{6,2},{... | collective-permute-start | bytes 786440 | tf_op jit(solution)/shard_map/ppermute | solution.py:37
  130.7 18.1 %collective-permute-start.34 = (bf16[512,256]{1,0:T(8,128)(2,1)S(1)}, bf16[512,256]{1,0:T(8,128)(2,1)S(1)}, u32[]{:S(2)}, u32[]{:S(2)}) collective-permute-start(bf16[512,256]{1,0:T(8,128)(2,1)S(1)} %add_in.6), channel_id=1, source_target_pairs={{0,4},{4,8},{8,12},{12,0},{1,5},{5,9},{9,13},{13,1},{2,6},{6,10},{... | collective-permute-start | bytes 786440 | tf_op jit(solution)/shard_map/ppermute | solution.py:37
  130.9 21.5 %collective-permute-start.30 = (bf16[512,256]{1,0:T(8,128)(2,1)S(1)}, bf16[512,256]{1,0:T(8,128)(2,1)S(1)}, u32[]{:S(2)}, u32[]{:S(2)}) collective-permute-start(bf16[512,256]{1,0:T(8,128)(2,1)S(1)} %add_in.5), channel_id=1, source_target_pairs={{0,12},{4,0},{8,4},{12,8},{1,13},{5,1},{9,5},{13,9},{2,14},{6,2},{... | collective-permute-start | bytes 786440 | tf_op jit(solution)/shard_map/ppermute | solution.py:37
  135.4 17.1 %collective-permute-start.26 = (bf16[512,256]{1,0:T(8,128)(2,1)S(1)}, bf16[512,256]{1,0:T(8,128)(2,1)S(1)}, u32[]{:S(2)}, u32[]{:S(2)}) collective-permute-start(bf16[512,256]{1,0:T(8,128)(2,1)S(1)} %add_in.4), channel_id=1, source_target_pairs={{0,4},{4,8},{8,12},{12,0},{1,5},{5,9},{9,13},{13,1},{2,6},{6,10},{... | collective-permute-start | bytes 786440 | tf_op jit(solution)/shard_map/ppermute | solution.py:37
  (26 other events, 231.1 us)
